TPU v7x, 32 devices: a whole 2x2x4 slice. The times are simulated.
32 devices in a mesh: grp: 2 (over y), lon: 4 (over z), lat: 2 (over x), lvl: 2 (over core).
Axes of the slice: x: 2, y: 2, z: 4, core: 2. Of those that a mesh axis runs over, the one named last changes fastest.
Arguments:
- tokens: bfloat16 [4, 24, 96, 512], P(('grp', 'lvl'), 'lat', 'lon'), parts along dimension 0, may hold values from -8 to 8
- fine_tags: int32 [4, 24, 96], P(('grp', 'lvl'), 'lat', 'lon'), parts along dimension 0, may hold values from 1 to 3
- coarse_tags: int32 [4, 12, 48], P(('grp', 'lvl'), 'lat', 'lon'), parts along dimension 0, may hold values from 1 to 3
- fine_gain: float32 [512], replicated, may hold values from 0.25 to 1.75
- fine_inward: bfloat16 [3, 512, 512], P(None, 'lon', 'lvl'), may hold values from -0.25 to 0.25
- fine_outward: bfloat16 [512, 512], P('lon', 'lvl'), may hold values from -0.25 to 0.25
- fine_table: float32 [16, 253], replicated, may hold values from -2 to 300
- merge_gain: float32 [2048], replicated, may hold values from 0.25 to 1.75
- merge_weight: bfloat16 [1024, 2048], P('lon', 'lvl'), may hold values from -0.125 to 0.125
- coarse_gain: float32 [1024], replicated, may hold values from 0.25 to 1.75
- coarse_inward: bfloat16 [3, 1024, 1024], P(None, 'lon', 'lvl'), may hold values from -0.1875 to 0.1875
- coarse_outward: bfloat16 [1024, 1024], P('lon', 'lvl'), may hold values from -0.1875 to 0.1875
- coarse_table: float32 [32, 253], replicated, may hold values from -2 to 300
Outputs:
- fine_out: bfloat16 [4, 24, 96, 512], P(('grp', 'lvl'), 'lat', 'lon'), parts along dimension 0
- coarse_out: bfloat16 [4, 12, 48, 1024], P(('grp', 'lvl'), 'lat', 'lon'), parts along dimension 0
There are 2 independent parts, one for each index of `grp`. A program takes and returns all parts, laid end to end along the dimension named above; an argument that names none is the same for every part. Nothing has to cross between parts.
All inputs are finite; a program needn't handle non-finite values.
Results may differ from a plain program's by a relative error of at most 0.017.
Values may be sent and summed in bfloat16 or wider, within the bound.
A program may use at most 64 MiB of HBM per device.

v0:
```python
import functools

import jax
import jax.numpy as jnp
import numpy as np
from jax import lax
from jax.experimental import pallas as pl
from jax.experimental.pallas import tpu as pltpu
from jax.sharding import PartitionSpec as P

WIN_LAT = 6
WIN_LON = 12
HALF_LAT = WIN_LAT // 2
HALF_LON = WIN_LON // 2
WIN = WIN_LAT * WIN_LON
EPSILON = 1e-05
LANES = 128
MESH = pl.DeviceIdType.MESH
VMEM = pl.BlockSpec(memory_space=pltpu.VMEM)
ANY = pl.BlockSpec(memory_space=pl.ANY)
LIMIT = 60 * 1024 * 1024
NT = (((1,), (1,)), ((), ()))
AROUND = ((0, -1), (0, 1), (-1, 0), (1, 0), (-1, -1), (-1, 1), (1, -1), (1, 1))


def up_to(count, step):
    return -(-count // step) * step


ROWS = up_to(WIN, 16)


class Plan:
    def __init__(self, lat_len, lon_len):
        self.lat_len, self.lon_len = lat_len, lon_len
        self.own = lat_len * lon_len
        self.own_rows = up_to(self.own, 16)
        self.segments = {}
        offset = self.own_rows
        for side in AROUND:
            count = self.extent(side)
            self.segments[side] = (offset, up_to(count, 16))
            offset += up_to(count, 16)
        self.wide_rows = offset
        self.bands = lat_len // WIN_LAT + 1
        self.columns = lon_len // WIN_LON + 1
        self.windows = self.bands * self.columns
        gather = np.full((self.windows * ROWS, 1), -1, np.int32)
        scatter = np.full((self.own_rows, 1), -1, np.int32)
        for w in range(self.windows):
            band, col = divmod(w, self.columns)
            for p in range(WIN):
                r = band * WIN_LAT - HALF_LAT + p // WIN_LON
                c = col * WIN_LON - HALF_LON + p % WIN_LON
                dy = -1 if r < 0 else int(r >= lat_len)
                dx = -1 if c < 0 else int(c >= lon_len)
                if dy == 0 and dx == 0:
                    gather[w * ROWS + p] = r * lon_len + c
                    scatter[r * lon_len + c] = w * ROWS + p
                    continue
                width = HALF_LON if dx else lon_len
                rr = r + HALF_LAT if dy < 0 else (r - lat_len if dy > 0 else r)
                cc = c + HALF_LON if dx < 0 else (c - lon_len if dx > 0 else c)
                gather[w * ROWS + p] = self.segments[(dy, dx)][0] + rr * width + cc
        self.gather, self.scatter = gather, scatter

    def extent(self, side):
        rows = HALF_LAT if side[0] else self.lat_len
        cols = HALF_LON if side[1] else self.lon_len
        return rows * cols

    def edges(self):
        result = np.full((self.wide_rows - self.own_rows, 1), -1, np.int32)
        for dy, dx in AROUND:
            offset = self.segments[(dy, dx)][0] - self.own_rows
            rows = range(self.lat_len)
            rows = rows[-HALF_LAT:] if dy < 0 else (rows[:HALF_LAT] if dy > 0 else rows)
            cols = range(self.lon_len)
            cols = cols[-HALF_LON:] if dx < 0 else (cols[:HALF_LON] if dx > 0 else cols)
            for i, (r, c) in enumerate((r, c) for r in rows for c in cols):
                result[offset + i] = r * self.lon_len + c
        return result

    def patches(self):
        half_lat, half_lon = self.lat_len // 2, self.lon_len // 2
        result = np.full((4, up_to(half_lat * half_lon, 16), 1), -1, np.int32)
        for s in range(2):
            for t in range(2):
                for a in range(half_lat):
                    for b in range(half_lon):
                        result[2 * s + t, a * half_lon + b] = (2 * a + s) * self.lon_len + 2 * b + t
        return result


def onehot(index, width):
    spots = lax.broadcasted_iota(jnp.int32, (index.shape[0], width), 1)
    return jnp.where(spots == index, 1.0, 0.0).astype(jnp.bfloat16)


def pick(index, source):
    return jnp.dot(
        onehot(index, source.shape[0]), source, preferred_element_type=jnp.float32
    ).astype(jnp.bfloat16)


def normalize(values, gain):
    widened = values.astype(jnp.float32)
    center = widened - jnp.mean(widened, axis=-1, keepdims=True)
    spread = jnp.mean(center * center, axis=-1, keepdims=True)
    return (center * lax.rsqrt(spread + EPSILON) * gain).astype(jnp.bfloat16)


def exchange_halo(plan, edge_ref, wide, send_sem, recv_sem, greeted=()):
    lat, lon = lax.axis_index("lat"), lax.axis_index("lon")
    lats, lons = lax.axis_size("lat"), lax.axis_size("lon")

    def place(dy, dx):
        return {"lat": lax.rem(lat + dy + lats, lats), "lon": lax.rem(lon + dx + lons, lons)}

    def when_there(dy, action):
        if dy == 0:
            action()
        else:
            pl.when((lat > 0) if dy < 0 else (lat < lats - 1))(action)

    barrier = pltpu.get_barrier_semaphore()
    for dy, dx in AROUND:
        def greet(dy=dy, dx=dx):
            pl.semaphore_signal(barrier, inc=1, device_id=place(dy, dx), device_id_type=MESH)
        when_there(dy, greet)
    peers = 2 + 3 * (lat > 0).astype(jnp.int32) + 3 * (lat < lats - 1).astype(jnp.int32)
    for device in greeted:
        pl.semaphore_signal(barrier, inc=1, device_id=device, device_id_type=MESH)
    pl.semaphore_wait(barrier, peers + len(greeted))

    def copy_of(number, dy, dx):
        offset, count = plan.segments[(dy, dx)]
        return pltpu.make_async_remote_copy(
            src_ref=edge_ref.at[pl.ds(offset - plan.own_rows, count)],
            dst_ref=wide.at[pl.ds(offset, count)],
            send_sem=send_sem.at[number],
            recv_sem=recv_sem.at[number],
            device_id=place(-dy, -dx),
            device_id_type=MESH,
        )

    for number, (dy, dx) in enumerate(AROUND):
        when_there(-dy, lambda n=number, y=dy, x=dx: copy_of(n, y, x).start())
        if dy:
            offset, count = plan.segments[(dy, dx)]

            def clear(offset=offset, count=count):
                wide[pl.ds(offset, count), :] = jnp.zeros((count, wide.shape[1]), wide.dtype)

            pl.when(jnp.logical_not((lat > 0) if dy < 0 else (lat < lats - 1)))(clear)

    def finish():
        for number, (dy, dx) in enumerate(AROUND):
            when_there(dy, lambda n=number, y=dy, x=dx: copy_of(n, y, x).wait_recv())
            when_there(-dy, lambda n=number, y=dy, x=dx: copy_of(n, y, x).wait_send())

    return finish


def fill_bias(number_ref, parts_ref, bias):
    heads = bias.shape[0]
    entries = parts_ref.shape[1]
    parts = parts_ref[...]
    spots = lax.broadcasted_iota(jnp.int32, (entries, LANES), 0)
    for p in range(WIN):
        hot = jnp.where(spots == number_ref[p : p + 1, :], 1.0, 0.0).astype(jnp.bfloat16)
        terms = jnp.dot(parts, hot, preferred_element_type=jnp.float32)
        bias[:, p, :] = terms[:heads] + terms[heads : 2 * heads] + terms[2 * heads :]
    bias[:, WIN:, :] = jnp.zeros((heads, ROWS - WIN, LANES), jnp.float32)


def arrange_windows(plan, wide, gather_ref, gain_ref, normed, tags):
    features = normed.shape[1]
    everything = wide[...]
    for w in range(plan.windows):
        rows = pl.ds(w * ROWS, ROWS)
        chosen = pick(gather_ref[rows, :], everything)
        normed[rows, :] = normalize(chosen[:, :features], gain_ref[...])
        tags[rows, :] = chosen[:, features:]


def attend_windows(plan, inward_ref, bias_ref, normed, triple, tags, mixed, unroll, after=None):
    features = normed.shape[1]
    heads = bias_ref.shape[0]
    size = features // heads
    per_group = LANES // size
    groups = features // LANES

    step = 256
    for member in range(3):
        @pl.loop(0, features // step)
        def _(block):
            cols = pl.ds(pl.multiple_of(block * step, step), step)
            triple[member, :, cols] = jnp.dot(
                normed[...], inward_ref[member, :, cols], preferred_element_type=jnp.float32
            ).astype(jnp.bfloat16)

    owner = lax.broadcasted_iota(jnp.int32, (ROWS, LANES), 1) // size
    fill = jnp.zeros((LANES - ROWS, LANES), jnp.bfloat16)
    first = jnp.where(
        lax.broadcasted_iota(jnp.int32, (16, LANES), 1) == 0, 1.0, 0.0
    ).astype(jnp.bfloat16)

    def spread(block):
        parts = []
        for h in range(per_group):
            parts += [jnp.where(owner == h, block, jnp.zeros_like(block)), fill]
        return jnp.concatenate(parts, axis=0)

    head_of_row = lax.broadcasted_iota(jnp.int32, (per_group * LANES, LANES), 0) // LANES
    head_of_lane = lax.broadcasted_iota(jnp.int32, (per_group * LANES, LANES), 1) // size
    ones = jnp.where(head_of_row == head_of_lane, 1.0, 0.0).astype(jnp.bfloat16)

    @pl.loop(0, plan.windows)
    def _(w):
        rows = pl.ds(pl.multiple_of(w * ROWS, ROWS), ROWS)
        tag_block = tags[rows, :]
        across = lax.dot_general(
            first, jnp.concatenate([tag_block, fill], axis=0), NT, preferred_element_type=jnp.float32
        )
        allowed = tag_block[:, :1].astype(jnp.float32) == across[:1, :]

        @pl.loop(0, groups, unroll=unroll)
        def _(g):
            cols = pl.ds(pl.multiple_of(g * LANES, LANES), LANES)
            scores = lax.dot_general(
                triple[0, rows, cols], spread(triple[1, rows, cols]), NT, preferred_element_type=jnp.float32
            )
            weights = []
            for h in range(per_group):
                score = scores[:, h * LANES : (h + 1) * LANES] * size ** (-0.5)
                score = score + bias_ref[g * per_group + h]
                score = jnp.where(allowed, score, -1e30)
                weight = jnp.exp(score - jnp.max(score, axis=-1, keepdims=True))
                weights.append(weight.astype(jnp.bfloat16))
            weights = jnp.concatenate(weights, axis=1)
            both = jnp.concatenate([spread(triple[2, rows, cols]), ones], axis=1)
            both = jnp.dot(weights, both, preferred_element_type=jnp.float32)
            blended, totals = both[:, :LANES], both[:, LANES:]
            mixed[rows, cols] = (blended / totals).astype(jnp.bfloat16)

        if after is not None:
            after(w)


def fine_kernel(
    plan, split, own_ref, edge_ref, tag_ref, gather_ref, scatter_ref, patch_ref, edge_index_ref, gain_ref,
    number_ref, parts_ref, coarse_parts_ref, merge_gain_ref, s0, s1, s2, s3, s4,
    fine_ref, coarse_ref, coarse_edge_ref, coarse_bias_ref, inward_two_ref, outward_two_ref,
    wide, normed, triple, tags, mixed, send_sem, recv_sem, bias_ref, inward_ref, outward_ref, merge_ref, *sems,
):
    features = normed.shape[1]
    shards = (s0, s1, s2, s3, s4)
    fulls = (inward_ref, outward_ref, merge_ref, inward_two_ref, outward_two_ref)
    gather = Gather(shards, fulls, split, sems)
    finish = exchange_halo(plan, edge_ref, wide, send_sem, recv_sem, gather.greeted())
    gather.begin()
    wide[: plan.own_rows, :] = own_ref[...]
    fill_bias(number_ref, parts_ref, bias_ref)
    finish()
    gather.step(0)
    arrange_windows(plan, wide, gather_ref, gain_ref, normed, tags)
    gather.step(1)
    gather.step(2)
    fill_bias(number_ref, coarse_parts_ref, coarse_bias_ref)
    gather.ready(0)
    last = gather.count + 2
    spots = {}
    for number in range(3, last):
        spots.setdefault(min((number - 3) * plan.windows // (last - 3) + 1, plan.windows - 1), []).append(number)

    def after(w):
        for spot, numbers in spots.items():
            @pl.when(w == spot)
            def _(numbers=numbers):
                for number in numbers:
                    gather.step(number)

    attend_windows(plan, inward_ref, bias_ref, normed, triple, tags, mixed, 4, after)
    gather.ready(1)
    own_mixed = pick(scatter_ref[...], mixed[...])
    update = lax.dot_general(own_mixed, outward_ref[0], NT, preferred_element_type=jnp.float32)
    fine = (own_ref[:, :features].astype(jnp.float32) + update).astype(jnp.bfloat16)
    fine_ref[...] = fine
    gather.ready(2)
    members = [pick(patch_ref[m], fine).astype(jnp.float32) for m in range(4)]
    count = 4 * features
    mean = sum(jnp.sum(m, axis=-1, keepdims=True) for m in members) / count
    centers = [m - mean for m in members]
    spread = sum(jnp.sum(c * c, axis=-1, keepdims=True) for c in centers) / count
    factor = lax.rsqrt(spread + EPSILON)
    merged = None
    for m in range(4):
        cols = slice(m * features, (m + 1) * features)
        part = (centers[m] * factor * merge_gain_ref[:, cols]).astype(jnp.bfloat16)
        term = lax.dot_general(part, merge_ref[0, :, cols], NT, preferred_element_type=jnp.float32)
        merged = term if merged is None else merged + term
    coarse = jnp.concatenate([merged.astype(jnp.bfloat16), tag_ref[...]], axis=1)
    coarse_ref[...] = coarse
    coarse_edge_ref[...] = pick(edge_index_ref[...], coarse)
    for number in range(3, gather.count):
        gather.ready(number)
    gather.end()


def coarse_kernel(
    plan, own_ref, edge_ref, gather_ref, scatter_ref, gain_ref, inward_ref, outward_ref, bias_ref,
    out_ref, wide, normed, triple, tags, mixed, send_sem, recv_sem,
):
    features = normed.shape[1]
    finish = exchange_halo(plan, edge_ref, wide, send_sem, recv_sem)
    wide[: plan.own_rows, :] = own_ref[...]
    finish()
    arrange_windows(plan, wide, gather_ref, gain_ref, normed, tags)
    attend_windows(plan, inward_ref, bias_ref, normed, triple, tags, mixed, 4)
    own_mixed = pick(scatter_ref[...], mixed[...])
    update = lax.dot_general(own_mixed, outward_ref[0], NT, preferred_element_type=jnp.float32)
    out_ref[...] = (own_ref[:, :features].astype(jnp.float32) + update).astype(jnp.bfloat16)


def level_scratch(plan, features):
    rows = plan.windows * ROWS
    return [
        pltpu.VMEM((plan.wide_rows, features + LANES), jnp.bfloat16),
        pltpu.VMEM((rows, features), jnp.bfloat16),
        pltpu.VMEM((3, rows, features), jnp.bfloat16),
        pltpu.VMEM((rows, LANES), jnp.bfloat16),
        pltpu.VMEM((rows, features), jnp.bfloat16),
        pltpu.SemaphoreType.DMA((len(AROUND),)),
        pltpu.SemaphoreType.DMA((len(AROUND),)),
    ]


class Gather:
    def __init__(self, shards, fulls, split, sems):
        self.shards, self.fulls, self.split, self.sems = shards, fulls, split, sems
        self.entries = weight_entries(shards)
        self.count = len(self.entries)
        self.index = {a: lax.axis_index(a) for a in ("grp", "lat", "lon", "lvl")}
        self.size = {a: lax.axis_size(a) for a in ("grp", "lat", "lon", "lvl")}
        self.halves = 2 if split else 1
        self.ways = [(d, half) for d in range(1, self.size["lon"]) for half in range(self.halves)]

    def at(self, axis, step):
        return {axis: lax.rem(self.index[axis] + step, self.size[axis])}

    def greeted(self):
        axes = ("lon", "lvl", "lat", "grp") if self.split else ("lon", "lvl")
        return [self.at(axis, d) for axis in axes for d in range(1, self.size[axis])]

    def place(self, n, lon_of, start, size):
        m, k, depth = self.entries[n]
        rows, cols = self.shards[m].shape[1:]
        return self.fulls[m].at[
            pl.ds(k, depth),
            pl.ds(pl.multiple_of(lon_of * rows + start, 16), size),
            pl.ds(pl.multiple_of(self.index["lvl"] * cols, cols), cols),
        ]

    def held(self, n, start, size):
        m, k, depth = self.entries[n]
        return self.shards[m].at[pl.ds(k, depth), pl.ds(start, size), :]

    def rows(self, n):
        return self.shards[self.entries[n][0]].shape[1]

    def source(self, d):
        return lax.rem(self.index["lon"] - d + self.size["lon"], self.size["lon"])

    def remote(self, src, dst, kind, number, device):
        send, recv = self.sems[1 + 2 * kind], self.sems[2 + 2 * kind]
        return pltpu.make_async_remote_copy(
            src_ref=src, dst_ref=dst, send_sem=send.at[number], recv_sem=recv.at[number],
            device_id=device, device_id_type=MESH,
        )

    def piece(self, n, half, grp_of, lat_of):
        rows = self.rows(n)
        if not self.split:
            return 0, rows
        grps, lats = self.size["grp"], self.size["lat"]
        size = rows // (2 * grps * lats)
        order = grp_of * lats + lat_of if half == 0 else lat_of * grps + grp_of
        start = half * (rows // 2) + order * size
        return pl.multiple_of(start, 16), size

    def mine(self, n, half):
        return self.piece(n, half, self.index["grp"], self.index["lat"])

    def axis_of(self, half, first):
        return "lat" if (half == 0) == first else "grp"

    def others(self, half, first):
        return range(1, self.size[self.axis_of(half, first)]) if self.split else ()

    def own_copy(self, n):
        return pltpu.make_async_copy(
            self.held(n, 0, self.rows(n)), self.place(n, self.index["lon"], 0, self.rows(n)), self.sems[0].at[n]
        )

    def lon_copy(self, n, d, half):
        start, size = self.mine(n, half)
        return self.remote(
            self.held(n, start, size), self.place(n, self.index["lon"], start, size),
            0, (n, d - 1, half), self.at("lon", d),
        )

    def one_copy(self, n, d, half, e):
        start, size = self.mine(n, half)
        block = self.place(n, self.source(d), start, size)
        return self.remote(block, block, 1, (n, d - 1, half, e - 1), self.at(self.axis_of(half, True), e))

    def two_copy(self, n, d, half, e):
        if half == 0:
            start, size = self.piece(n, half, self.index["grp"], 0)
            size *= self.size["lat"]
        else:
            start, size = self.piece(n, half, 0, self.index["lat"])
            size *= self.size["grp"]
        block = self.place(n, self.source(d), start, size)
        return self.remote(block, block, 2, (n, d - 1, half, e - 1), self.at(self.axis_of(half, False), e))

    def lvl_copy(self, n, d, e):
        block = self.place(n, self.source(d), 0, self.rows(n))
        src = block if d else self.held(n, 0, self.rows(n))
        return self.remote(src, block, 3, (n, d, e - 1), self.at("lvl", e))

    def siblings(self):
        return range(1, self.size["lvl"])

    def begin(self):
        for n in range(self.count):
            self.own_copy(n).start()
            for d, half in self.ways:
                self.lon_copy(n, d, half).start()
            for e in self.siblings():
                self.lvl_copy(n, 0, e).start()

    def step(self, s):
        if s < self.count:
            for d, half in self.ways:
                self.lon_copy(s, d, half).wait_recv()
                for e in self.others(half, True):
                    self.one_copy(s, d, half, e).start()
        if 0 <= s - 1 < self.count:
            for d, half in self.ways:
                for e in self.others(half, True):
                    self.one_copy(s - 1, d, half, e).wait_recv()
                for e in self.others(half, False):
                    self.two_copy(s - 1, d, half, e).start()
        if 0 <= s - 2 < self.count:
            for d in range(1, self.size["lon"]):
                for half in range(self.halves):
                    for e in self.others(half, False):
                        self.two_copy(s - 2, d, half, e).wait_recv()
                for e in self.siblings():
                    self.lvl_copy(s - 2, d, e).start()

    def ready(self, n):
        self.own_copy(n).wait()
        for d in range(self.size["lon"]):
            for e in self.siblings():
                self.lvl_copy(n, d, e).wait_recv()

    def end(self):
        for n in range(self.count):
            for d in range(self.size["lon"]):
                for e in self.siblings():
                    self.lvl_copy(n, d, e).wait_send()
            for d, half in self.ways:
                self.lon_copy(n, d, half).wait_send()
                for e in self.others(half, True):
                    self.one_copy(n, d, half, e).wait_send()
                for e in self.others(half, False):
                    self.two_copy(n, d, half, e).wait_send()


def weight_entries(weights):
    result = []
    for m, w in enumerate(weights):
        each = w.shape[0] if m == 0 else 1
        result += [(m, k, each) for k in range(0, w.shape[0], each)]
    return result


def gather_scratch(weights, split):
    grps, lats, lons, lvls = (lax.axis_size(a) for a in ("grp", "lat", "lon", "lvl"))
    count = len(weight_entries(weights))
    halves = 2 if split else 1
    most = max(grps, lats) - 1 if split else 1
    dma = pltpu.SemaphoreType.DMA
    return (
        [dma((count,))]
        + [dma((count, lons - 1, halves))] * 2
        + [dma((count, lons - 1, halves, most))] * 4
        + [dma((count, lons, lvls - 1))] * 2
    )


def offset_numbers():
    p = np.arange(WIN)
    r, c = p // WIN_LON, p % WIN_LON
    number = (r[:, None] - r[None, :] + WIN_LAT - 1) * (2 * WIN_LON - 1) + c[:, None] - c[None, :] + WIN_LON - 1
    result = np.full((ROWS, LANES), -1, np.int32)
    result[:WIN, :WIN] = number
    return result


def table_parts(table):
    terms, rest = [], table
    for _ in range(3):
        term = lax.reduce_precision(rest, 8, 7)
        terms.append(term.astype(jnp.bfloat16))
        rest = rest - term
    parts = jnp.concatenate(terms, axis=0)
    return jnp.pad(parts, ((0, 0), (0, up_to(parts.shape[1], LANES) - parts.shape[1])))


def shards(
    tokens, fine_tags, coarse_tags, fine_gain, fine_inward, fine_outward, fine_table, merge_gain,
    merge_weight, coarse_gain, coarse_inward, coarse_outward, coarse_table,
):
    _, lat_len, lon_len, width = tokens.shape
    fine_plan, coarse_plan = Plan(lat_len, lon_len), Plan(lat_len // 2, lon_len // 2)
    weights = [fine_inward, fine_outward[None], merge_weight[None], coarse_inward, coarse_outward[None]]
    grps, lats, lons, lvls = (lax.axis_size(a) for a in ("grp", "lat", "lon", "lvl"))
    split = all(w.shape[1] % (2 * grps * lats * 16) == 0 for w in weights)
    wholes = [(w.shape[0], w.shape[1] * lons, w.shape[2] * lvls) for w in weights]

    tagged = jnp.concatenate(
        [tokens[0], jnp.broadcast_to(fine_tags[0, :, :, None], (lat_len, lon_len, LANES)).astype(jnp.bfloat16)], axis=2
    )
    own = tagged.reshape(lat_len * lon_len, -1)
    own = jnp.pad(own, ((0, fine_plan.own_rows - fine_plan.own), (0, 0)))
    pieces = []
    for dy, dx in AROUND:
        part = tagged
        part = part[-HALF_LAT:] if dy < 0 else (part[:HALF_LAT] if dy > 0 else part)
        part = part[:, -HALF_LON:] if dx < 0 else (part[:, :HALF_LON] if dx > 0 else part)
        part = part.reshape(-1, part.shape[2])
        pieces.append(jnp.pad(part, ((0, up_to(part.shape[0], 16) - part.shape[0]), (0, 0))))
    edge = jnp.concatenate(pieces, axis=0)
    coarse_width = wholes[2][1]
    coarse_marks = jnp.broadcast_to(coarse_tags.reshape(-1, 1), (coarse_plan.own, LANES)).astype(jnp.bfloat16)
    coarse_marks = jnp.pad(coarse_marks, ((0, coarse_plan.own_rows - coarse_plan.own), (0, 0)))

    edge_rows = coarse_plan.wide_rows - coarse_plan.own_rows
    heads, coarse_heads = fine_table.shape[0], coarse_table.shape[0]
    fine, coarse_own, coarse_edge, coarse_bias, inward_two, outward_two = pl.pallas_call(
        functools.partial(fine_kernel, fine_plan, split),
        out_shape=[
            jax.ShapeDtypeStruct((fine_plan.own_rows, width), jnp.bfloat16),
            jax.ShapeDtypeStruct((coarse_plan.own_rows, coarse_width + LANES), jnp.bfloat16),
            jax.ShapeDtypeStruct((edge_rows, coarse_width + LANES), jnp.bfloat16),
            jax.ShapeDtypeStruct((coarse_heads, ROWS, LANES), jnp.float32),
            jax.ShapeDtypeStruct(wholes[3], jnp.bfloat16),
            jax.ShapeDtypeStruct(wholes[4], jnp.bfloat16),
        ],
        in_specs=[VMEM] * 12 + [ANY] * 5,
        out_specs=[VMEM] * 6,
        scratch_shapes=level_scratch(fine_plan, width)
        + [pltpu.VMEM((heads, ROWS, LANES), jnp.float32)]
        + [pltpu.VMEM(shape, jnp.bfloat16) for shape in wholes[:3]]
        + gather_scratch(weights, split),
        compiler_params=pltpu.CompilerParams(collective_id=1, has_side_effects=True, vmem_limit_bytes=LIMIT),
        name="fine_level",
    )(
        own, edge, coarse_marks, fine_plan.gather, fine_plan.scatter, fine_plan.patches(),
        coarse_plan.edges(), fine_gain[None], offset_numbers(), table_parts(fine_table),
        table_parts(coarse_table), merge_gain[None], *weights,
    )
    coarse = pl.pallas_call(
        functools.partial(coarse_kernel, coarse_plan),
        out_shape=jax.ShapeDtypeStruct((coarse_plan.own_rows, coarse_width), jnp.bfloat16),
        in_specs=[VMEM] * 8,
        out_specs=VMEM,
        scratch_shapes=level_scratch(coarse_plan, coarse_width),
        compiler_params=pltpu.CompilerParams(collective_id=2, has_side_effects=True, vmem_limit_bytes=LIMIT),
        name="coarse_level",
    )(
        coarse_own, coarse_edge, coarse_plan.gather, coarse_plan.scatter, coarse_gain[None],
        inward_two, outward_two, coarse_bias,
    )
    fine = fine[: fine_plan.own].reshape(tokens.shape)
    coarse = coarse[: coarse_plan.own].reshape(1, lat_len // 2, lon_len // 2, coarse_width)
    return fine, coarse


def solution(mesh):
    placed = (
        P(("grp", "lvl"), "lat", "lon", None),
        P(("grp", "lvl"), "lat", "lon"),
        P(("grp", "lvl"), "lat", "lon"),
        P(),
        P(None, "lon", "lvl"),
        P("lon", "lvl"),
        P(),
        P(),
        P("lon", "lvl"),
        P(),
        P(None, "lon", "lvl"),
        P("lon", "lvl"),
        P(),
    )
    return jax.shard_map(
        shards,
        mesh=mesh,
        in_specs=placed,
        out_specs=(P(("grp", "lvl"), "lat", "lon", None), P(("grp", "lvl"), "lat", "lon", None)),
        check_vma=False,
    )
```

profile of v0, /device:TPU:0, one launch (start us, length us, event | category | flops | bytes accessed | tf_op | source)
XLA Modules:
  0.0 138.3 jit_solution(13077546952395385548)
XLA Ops:
  0.6 0.0 copy-start
  0.6 0.7 convert_reduce_fusion
  1.4 0.1 convert_element_type.56
  1.5 0.7 convert_reduce_fusion.1
  2.2 0.1 convert_element_type.53
  2.3 0.7 convert_element_type.52
  3.0 0.7 pad.49.tag_ref
  3.7 0.7 reduce-precision_convert_fusion.3
  4.4 0.6 fusion.18.parts_ref
  5.0 0.8 reduce-precision_convert_fusion.1
  5.8 0.6 fusion.8.coarse_parts_ref
  6.5 0.1 broadcast_in_dim.29
  6.6 0.1 broadcast_in_dim.28
  6.7 0.8 pad_maximum_fusion.1
  7.6 0.9 fusion.6
  8.5 1.0 fusion.1
  9.6 0.0 copy-done
  9.6 0.8 pad_maximum_fusion.own_ref
  10.5 0.0 copy-start.1
  10.6 0.8 copy-done.1
  11.4 89.7 %fine_level.1 = (bf16[288,512]{1,0:T(8,128)(2,1)}, bf16[80,1152]{1,0:T(8,128)(2,1)}, bf16[320,1152]{1,0:T(8,128)(2,1)}, f32[32,80,128]{2,1,0:T(8,128)}, bf16[3,1...) custom-call(bf16[288,640]{1,0:T(8,128)(2,1)} %pad_maximum_fusion.own_ref, bf16[448,640]{1,0:T(8,128)(2,1)} %copy-done.1, ...), custom_call_target="tpu_custom_call" | custom-call | tf_op jit(solution)/shard_map/fine_level/pallas_call | solution.py:554
  101.1 0.0 copy-start.2
  101.1 34.9 %coarse_level.1 = bf16[80,1024]{1,0:T(8,128)(2,1)} custom-call(bf16[80,1152]{1,0:T(8,128)(2,1)} %get-tuple-element.9.own_ref, bf16[320,1152]{1,0:T(8,128)(2,1)} %get-tuple-element.10.edge_ref, s32[320,1]{1,0:T(8,128)} %constant.22.clone.gather_ref, s32[80,1]{1,0:T(8,128)} %constant.23.clone.scatter_ref, f32[1,1024]{1,0:T(1,128)} %bitcast.26, ...), custom_call_target="tpu_custom_call" | custom-call | tf_op jit(solution)/shard_map/coarse_level/pallas_call | solution.py:577
  136.0 0.9 slice.43
  136.9 0.7 reshape.55
  137.6 0.0 copy-done.2
  137.6 0.7 copy.33
  (16 shorter events, 0.3 us)
Async XLA Ops:
  0.6 9.0 %copy-start = (bf16[1,12,24,512]{3,2,1,0:T(8,128)(2,1)S(1)}, bf16[1,12,24,512]{3,2,1,0:T(8,128)(2,1)}, u32[]{:S(2)}) copy-start(bf16[1,12,24,512]{3,2,1,0:T(8,128)(2,1)} %param.20) | copy-start | bytes 884740
  10.5 0.8 copy-start.1
  101.1 36.5 %copy-start.2 = (bf16[288,512]{1,0:T(8,128)(2,1)S(1)}, bf16[288,512]{1,0:T(8,128)(2,1)}, u32[]{:S(2)}) copy-start(bf16[288,512]{1,0:T(8,128)(2,1)} %get-tuple-element.8) | copy-start | bytes 884740
where the time goes:
time: 139 us; the launch traced here: 138 us
  Pallas kernels  125 us (90%)
  other arithmetic  8.45 us (6%)
  local copies, waits for them, and re-layouts  4.51 us (3%)
    pallas_call x1, Pallas kernels, shards(): pl.pallas_call(functools.partial(fine_kernel, fine_plan, split), out_shap...  89.7 us
    pallas_call x1, Pallas kernels, shards(): pl.pallas_call(functools.partial(coarse_kernel, coarse_plan), out_shape=j...  34.9 us
    concatenate x4, other arithmetic, shards(): jnp.concatenate([tokens[0], jnp.broadcast_to(fine_tags[0, :, :, None], (l...  3.53 us

commit v1 on v0

v1 whole, which is shorter than its diff:
```python
import functools
import math

import jax
import jax.numpy as jnp
import numpy as np
from jax import lax
from jax.experimental import pallas as pl
from jax.experimental.pallas import tpu as pltpu
from jax.sharding import PartitionSpec as P

WIN_LAT = 6
WIN_LON = 12
HALF_LAT = WIN_LAT // 2
HALF_LON = WIN_LON // 2
QUAD = HALF_LAT * HALF_LON
ROWS = -(-QUAD // 16) * 16
WINDOW = 4 * ROWS
EPSILON = 1e-05
LANES = 128
LOG2E = math.log2(math.e)
MESH = pl.DeviceIdType.MESH
VMEM = pl.BlockSpec(memory_space=pltpu.VMEM)
ANY = pl.BlockSpec(memory_space=pl.ANY)
LIMIT = 60 * 1024 * 1024
NT = (((1,), (1,)), ((), ()))
AROUND = ((0, -1), (0, 1), (-1, 0), (1, 0), (-1, -1), (-1, 1), (1, -1), (1, 1))
AHEAD = 2


def up_to(count, step):
    return -(-count // step) * step


class Plan:
    def __init__(self, lat_len, lon_len):
        self.lat_len, self.lon_len = lat_len, lon_len
        self.own = lat_len * lon_len
        self.down, self.across = lat_len // HALF_LAT, lon_len // HALF_LON
        self.quads = self.down * self.across
        self.columns = self.across // 2 + 1
        self.windows = (self.down // 2 + 1) * self.columns
        self.halo = []
        for side, (dy, dx) in enumerate(AROUND):
            rows = [-1] if dy < 0 else ([self.down] if dy > 0 else range(self.down))
            cols = [-1] if dx < 0 else ([self.across] if dx > 0 else range(self.across))
            for r in rows:
                for c in cols:
                    self.halo.append((side, r, c, (r % self.down) * self.across + c % self.across))

    def spot(self, r, c):
        window = ((r + 1) // 2) * self.columns + (c + 1) // 2
        return 4 * window + ((r + 1) % 2) * 2 + (c + 1) % 2

    def natural(self):
        result = np.full((self.quads * ROWS,), -1, np.int32)
        for q in range(self.quads):
            for p in range(QUAD):
                r = (q // self.across) * HALF_LAT + p // HALF_LON
                c = (q % self.across) * HALF_LON + p % HALF_LON
                result[q * ROWS + p] = r * self.lon_len + c
        return result

    def back(self, pitch):
        result = np.full((self.lat_len * pitch,), -1, np.int32)
        for row, token in enumerate(self.natural()):
            if token >= 0:
                result[token // self.lon_len * pitch + token % self.lon_len] = row
        return result

    def lanes(self):
        lane = np.arange(self.across * LANES)
        place = lane % ROWS
        column = (lane // LANES) * HALF_LON + place % HALF_LON
        return np.where(place < QUAD, column, -1), np.where(place < QUAD, place // HALF_LON, -1)


def patches(fine, coarse):
    token = coarse.natural()
    result = []
    for s in range(2):
        for t in range(2):
            a, b = token // coarse.lon_len, token % coarse.lon_len
            result.append(np.where(token >= 0, (2 * a + s) * fine.lon_len + 2 * b + t, -1))
    return np.concatenate(result)


def offset_numbers():
    spot = np.arange(WINDOW)
    place = spot % ROWS
    r = spot // ROWS // 2 * HALF_LAT + place // HALF_LON
    c = spot // ROWS % 2 * HALF_LON + place % HALF_LON
    number = (r[:, None] - r[None, :] + WIN_LAT - 1) * (2 * WIN_LON - 1) + c[:, None] - c[None, :] + WIN_LON - 1
    valid = (place < QUAD)[:, None] & (place < QUAD)[None, :]
    return np.where(valid, number, -1).astype(np.int32)


def onehot(index, width):
    spots = lax.broadcasted_iota(jnp.int32, (index.shape[0], width), 1)
    return jnp.where(spots == index, 1.0, 0.0).astype(jnp.bfloat16)


def pick(index, source):
    return jnp.dot(
        onehot(index, source.shape[0]), source, preferred_element_type=jnp.float32
    ).astype(jnp.bfloat16)


def normalize(values, gain):
    widened = values.astype(jnp.float32)
    center = widened - jnp.mean(widened, axis=-1, keepdims=True)
    spread = jnp.mean(center * center, axis=-1, keepdims=True)
    return (center * lax.rsqrt(spread + EPSILON) * gain).astype(jnp.bfloat16)


class Around:
    def __init__(self):
        self.lat, self.lon = lax.axis_index("lat"), lax.axis_index("lon")
        self.lats, self.lons = lax.axis_size("lat"), lax.axis_size("lon")

    def place(self, dy, dx):
        return {
            "lat": lax.rem(self.lat + dy + self.lats, self.lats),
            "lon": lax.rem(self.lon + dx + self.lons, self.lons),
        }

    def there(self, dy):
        return (self.lat > 0) if dy < 0 else (self.lat < self.lats - 1)

    def when_there(self, dy, action):
        if dy == 0:
            action()
        else:
            pl.when(self.there(dy))(action)

    def greet(self, barrier):
        for dy, dx in AROUND:
            def signal(dy=dy, dx=dx):
                pl.semaphore_signal(barrier, inc=1, device_id=self.place(dy, dx), device_id_type=MESH)
            self.when_there(dy, signal)
        return 2 + 3 * (self.lat > 0).astype(jnp.int32) + 3 * (self.lat < self.lats - 1).astype(jnp.int32)

    def copy(self, src, dst, send, recv, dy, dx):
        return pltpu.make_async_remote_copy(
            src_ref=src, dst_ref=dst, send_sem=send, recv_sem=recv,
            device_id=self.place(-dy, -dx), device_id_type=MESH,
        )


class Halo:
    def __init__(self, around, plan, own, wide, send, recv):
        self.around, self.plan, self.own, self.wide, self.send, self.recv = around, plan, own, wide, send, recv

    def copy(self, n):
        side, r, c, q = self.plan.halo[n]
        return self.around.copy(
            self.own.at[pl.ds(q * ROWS, ROWS)], self.wide.at[pl.ds(self.plan.spot(r, c) * ROWS, ROWS)],
            self.send.at[n], self.recv.at[n], *AROUND[side],
        )

    def start(self):
        for n, (side, r, c, _) in enumerate(self.plan.halo):
            dy = AROUND[side][0]
            self.around.when_there(-dy, lambda n=n: self.copy(n).start())
            if dy:
                def clear(r=r, c=c):
                    rows = pl.ds(self.plan.spot(r, c) * ROWS, ROWS)
                    self.wide[rows, :] = jnp.zeros((ROWS, self.wide.shape[1]), self.wide.dtype)
                pl.when(jnp.logical_not(self.around.there(dy)))(clear)

    def finish(self):
        for n, (side, *_) in enumerate(self.plan.halo):
            self.around.when_there(AROUND[side][0], lambda n=n: self.copy(n).wait_recv())

    def drain(self):
        for n, (side, *_) in enumerate(self.plan.halo):
            self.around.when_there(-AROUND[side][0], lambda n=n: self.copy(n).wait_send())


class Gather:
    def __init__(self, shards, fulls, units, split, sems):
        self.shards, self.fulls, self.units, self.split, self.sems = shards, fulls, units, split, sems
        self.index = {a: lax.axis_index(a) for a in ("grp", "lat", "lon", "lvl")}
        self.size = {a: lax.axis_size(a) for a in ("grp", "lat", "lon", "lvl")}
        self.halves = range(2 if split else 1)
        self.ways = [(s, half) for s in range(1, self.size["lon"]) for half in self.halves]
        self.now = 0
        self.steps = len(units) + (2 if split else 0)

    def at(self, axis, step):
        return {axis: lax.rem(self.index[axis] + step + self.size[axis], self.size[axis])}

    def greet(self, barrier):
        peers = 0
        for axis in ("lon", "lvl", "lat", "grp") if self.split else ("lon", "lvl"):
            for d in range(1, self.size[axis]):
                pl.semaphore_signal(barrier, inc=1, device_id=self.at(axis, d), device_id_type=MESH)
                peers += 1
        return peers

    def block_of(self, slot):
        return lax.rem(self.index["lon"] + slot, self.size["lon"]) if self.split else slot

    def rows(self, u):
        return self.shards[self.units[u][0]].shape[1]

    def axes(self, half):
        return ("lat", "grp") if half == 0 else ("grp", "lat")

    def piece(self, u, half):
        if not self.split:
            return 0, self.rows(u)
        size = self.rows(u) // 8
        first, second = self.axes(half)
        order = self.index[second] * 2 + self.index[first]
        return pl.multiple_of((half * 4 + order) * size, 16), size

    def pair(self, u, half):
        size = self.rows(u) // 8
        return pl.multiple_of((half * 4 + self.index[self.axes(half)[1]] * 2) * size, 16), 2 * size

    def held(self, u, start, size):
        m, k, depth, col, cols = self.units[u]
        return self.shards[m].at[pl.ds(k, depth), pl.ds(start, size), pl.ds(col, cols)]

    def block(self, u, slot, slots, start, size):
        m, k, depth, col, cols = self.units[u]
        return self.fulls[m].at[
            self.index["lvl"], pl.ds(k, depth), pl.ds(slot, slots), pl.ds(start, size), pl.ds(col, cols)
        ]

    def slot(self, u, slot, start, size):
        m, k, depth, col, cols = self.units[u]
        return self.fulls[m].at[self.index["lvl"], pl.ds(k, depth), slot, pl.ds(start, size), pl.ds(col, cols)]

    def remote(self, src, dst, kind, number, device):
        send, recv = self.sems[1 + 2 * kind], self.sems[2 + 2 * kind]
        return pltpu.make_async_remote_copy(
            src_ref=src, dst_ref=dst, send_sem=send.at[number], recv_sem=recv.at[number],
            device_id=device, device_id_type=MESH,
        )

    def own_copy(self, u):
        slot = 0 if self.split else self.index["lon"]
        return pltpu.make_async_copy(
            self.held(u, 0, self.rows(u)), self.slot(u, slot, 0, self.rows(u)), self.sems[0].at[u]
        )

    def lon_copy(self, u, s, half):
        start, size = self.piece(u, half)
        slot = s if self.split else self.index["lon"]
        return self.remote(
            self.held(u, start, size), self.slot(u, slot, start, size), 0, (u, s - 1, half), self.at("lon", -s)
        )

    def one_copy(self, u, half):
        block = self.block(u, 1, self.size["lon"] - 1, *self.piece(u, half))
        return self.remote(block, block, 1, (u, half), self.at(self.axes(half)[0], 1))

    def two_copy(self, u, half):
        block = self.block(u, 1, self.size["lon"] - 1, *self.pair(u, half))
        return self.remote(block, block, 2, (u, half), self.at(self.axes(half)[1], 1))

    def lvl_copy(self, u):
        block = self.block(u, 0, self.size["lon"], 0, self.rows(u))
        return self.remote(block, block, 3, (u,), self.at("lvl", 1))

    def issue(self, u):
        if u < len(self.units):
            for s, half in self.ways:
                self.lon_copy(u, s, half).start()
            self.own_copy(u).start()

    def begin(self):
        for u in range(AHEAD):
            self.issue(u)

    def step(self):
        k, count = self.now, len(self.units)
        self.now += 1
        if k < count:
            for half in self.halves:
                for s in range(1, self.size["lon"]):
                    self.lon_copy(k, s, half).wait_recv()
                if self.split:
                    self.one_copy(k, half).start()
            self.issue(k + AHEAD)
        if self.split and 0 <= k - 1 < count:
            for half in self.halves:
                self.one_copy(k - 1, half).wait_recv()
                self.two_copy(k - 1, half).start()
        done = k - 2 if self.split else k
        if 0 <= done < count:
            if self.split:
                for half in self.halves:
                    self.two_copy(done, half).wait_recv()
            self.own_copy(done).wait()
            self.lvl_copy(done).start()

    def ready(self, *wanted):
        for u in wanted:
            while self.now <= u + (2 if self.split else 0):
                self.step()
            self.lvl_copy(u).wait_recv()

    def end(self):
        for u in range(len(self.units)):
            self.lvl_copy(u).wait_send()
            for s, half in self.ways:
                self.lon_copy(u, s, half).wait_send()
            if self.split:
                for half in self.halves:
                    self.one_copy(u, half).wait_send()
                    self.two_copy(u, half).wait_send()


def weight_units(shards):
    fine_inward, fine_outward, merge, coarse_inward, coarse_outward = [s.shape for s in shards]
    units = [(0, k, 1, 0, fine_inward[2]) for k in range(3)]
    units.append((1, 0, 1, 0, fine_outward[2]))
    units += [(2, 0, 1, c, merge[2] // 4) for c in range(0, merge[2], merge[2] // 4)]
    units += [(3, 0, 3, c, LANES) for c in range(0, coarse_inward[2], LANES)]
    half = coarse_outward[2] // 2
    units += [(4, 0, 1, c, half) for c in (0, half)]
    return units


def gather_scratch(units, split):
    count, lons = len(units), lax.axis_size("lon")
    halves = 2 if split else 1
    dma = pltpu.SemaphoreType.DMA
    return (
        [dma((count,))] + [dma((count, lons - 1, halves))] * 2 + [dma((count, halves))] * 4 + [dma((count,))] * 2
    )


def flat(block):
    return block.reshape(block.shape[0] * block.shape[1], block.shape[2])


def turned(ref, rows, block_of, slots):
    size = ref.shape[1] // slots
    if size % LANES:
        return ref[rows, :]
    return jnp.concatenate(
        [ref[rows, pl.ds(pl.multiple_of(block_of(s) * size, size), size)] for s in range(slots)], axis=1
    )


def turn_back(value, block_of, slots, store):
    size = value.shape[1] // slots
    if size % LANES:
        store(slice(None), value)
        return
    for s in range(slots):
        store(pl.ds(pl.multiple_of(block_of(s) * size, size), size), value[:, s * size : (s + 1) * size])


def tag_rows(plan, tags_ref, column, place, features):
    grid = jnp.concatenate([tags_ref[r].astype(jnp.float32) for r in range(plan.lat_len)], axis=0)
    spots = lax.broadcasted_iota(jnp.int32, (plan.lon_len, features), 0)
    hot = jnp.where(spots == column, 1.0, 0.0).astype(jnp.bfloat16)
    spread = jnp.dot(grid.astype(jnp.bfloat16), hot, preferred_element_type=jnp.float32)
    rows = []
    for q in range(plan.down):
        row = jnp.zeros((1, features), jnp.float32)
        for k in range(HALF_LAT):
            r = q * HALF_LAT + k
            row = jnp.where(place == k, spread[r : r + 1, :], row)
        rows.append(row)
    return jnp.concatenate(rows, axis=0)


def fill_masks(plan, tags, offset, masks):
    lane = lax.broadcasted_iota(jnp.int32, (ROWS, LANES), 1)
    row = lax.broadcasted_iota(jnp.int32, (ROWS, LANES), 0)
    owner = lax.broadcasted_iota(jnp.int32, (1, LANES), 1) // ROWS

    def tag_row(r, c):
        dy = -1 if r < 0 else int(r >= plan.down)
        dx = -1 if c < 0 else int(c >= plan.across)
        side = AROUND.index((dy, dx)) if dy or dx else len(AROUND)
        r, c = r % plan.down, c % plan.across
        return tags[side][r : r + 1, offset + c * LANES : offset + (c + 1) * LANES]

    for q in range(plan.quads):
        r, c = divmod(q, plan.across)
        top, left = r - (r + 1) % 2, c - (c + 1) % 2
        across = tag_row(top, left)
        for a in range(1, 4):
            across = jnp.where(owner == a, tag_row(top + a // 2, left + a % 2), across)
        down = jnp.sum(jnp.where(lane == row, tag_row(r, c), 0.0), axis=-1, keepdims=True)
        masks[q] = jnp.where(down == across, 0.0, -1e30)


def split_table(tables, padded):
    padded[...] = jnp.zeros_like(padded)
    start = 0
    for table in tables:
        heads, entries = table.shape
        padded[start : start + heads, :entries] = table[...] * LOG2E
        start += heads
    rest, terms = padded[...], []
    for _ in range(3):
        term = rest.astype(jnp.bfloat16)
        terms.append(term)
        rest = rest - term.astype(jnp.float32)
    return jnp.concatenate(terms, axis=0)


def fill_bias(parts, number_ref, biases, first, last):
    total = parts.shape[0] // 3
    spots = lax.broadcasted_iota(jnp.int32, (parts.shape[1], LANES), 0)
    for p in range(first, last):
        row = p // QUAD * ROWS + p % QUAD
        hot = jnp.where(spots == number_ref[row : row + 1, :], 1.0, 0.0).astype(jnp.bfloat16)
        terms = jnp.dot(parts, hot, preferred_element_type=jnp.float32)
        value = terms[:total] + terms[total : 2 * total] + terms[2 * total :]
        start = 0
        for bias in biases:
            bias[:, row, :] = value[start : start + bias.shape[0]]
            start += bias.shape[0]


def attend(plan, q, group, query, keys, values, bias_ref, masks, mixed, size):
    heads = LANES // size
    r = lax.div(q, plan.across)
    c = q - r * plan.across
    window = lax.div(r + 1, 2) * plan.columns + lax.div(c + 1, 2)
    place = lax.rem(r + 1, 2) * 2 + lax.rem(c + 1, 2)
    rows = pl.ds(pl.multiple_of(q * ROWS, ROWS), ROWS)
    others = pl.ds(pl.multiple_of(window * WINDOW, WINDOW), WINDOW)
    inside = pl.ds(pl.multiple_of(place * ROWS, ROWS), ROWS)
    cols = slice(group * LANES, (group + 1) * LANES)
    owner = lax.broadcasted_iota(jnp.int32, (ROWS, LANES), 1) // size
    block = query[rows, cols]
    stack = jnp.concatenate([jnp.where(owner == h, block, jnp.zeros_like(block)) for h in range(heads)], axis=0)
    scores = lax.dot_general(stack, keys[others, cols], NT, preferred_element_type=jnp.float32)
    mask = masks[q]
    weights = []
    for h in range(heads):
        score = scores[h * ROWS : (h + 1) * ROWS] + bias_ref[group * heads + h, inside, :] + mask
        weights.append(jnp.exp2(score - jnp.max(score, axis=-1, keepdims=True)).astype(jnp.bfloat16))
    weights = jnp.concatenate(weights, axis=0)
    ones = jnp.ones((WINDOW, LANES), jnp.bfloat16)
    both = jnp.dot(weights, jnp.concatenate([values[others, cols], ones], axis=1), preferred_element_type=jnp.float32)
    result = both[:ROWS]
    blended, totals = result[:, :LANES], result[:, LANES:]
    for h in range(1, heads):
        result = both[h * ROWS : (h + 1) * ROWS]
        blended = jnp.where(owner == h, result[:, :LANES], blended)
        totals = jnp.where(owner == h, result[:, LANES:], totals)
    mixed[rows, cols] = (blended / totals).astype(jnp.bfloat16)


def kernel(
    fine, coarse, units, split, tokens_ref, fine_tags, coarse_tags, fine_gain, merge_gain, coarse_gain, fine_table,
    coarse_table, index_ref, number_ref, lane_ref, s0, s1, s2, s3, s4, fine_ref, coarse_ref,
    tokens, own, wide, query, keys, values, mixed, fine_bias, fine_masks, fine_value,
    two_own, two_wide, two_query, two_keys, two_values, two_mixed, coarse_bias, coarse_masks, two_in, two_value,
    padded, tag_own, tag_wide, f0, f1, f2, f3, f4, local, tag_send, tag_recv, send1, recv1, send2, recv2, *sems,
):
    width, wide_two = tokens.shape[1], two_own.shape[1]
    heads, heads_two = fine_bias.shape[0], coarse_bias.shape[0]
    size = width // heads
    scale = size ** (-0.5) * LOG2E
    around = Around()
    lons, lvls = lax.axis_size("lon"), lax.axis_size("lvl")
    gather = Gather((s0, s1, s2, s3, s4), (f0, f1, f2, f3, f4), units, split, sems)
    block_of = gather.block_of
    fetch = pltpu.make_async_copy(tokens_ref, tokens, local.at[0])
    fetch.start()
    tag_wide[...] = jnp.zeros_like(tag_wide)
    barrier = pltpu.get_barrier_semaphore()
    peers = around.greet(barrier) + gather.greet(barrier)

    fine_lanes = fine.across * LANES
    coarse_lanes = coarse.across * LANES
    tag_own[...] = jnp.zeros_like(tag_own)
    top = tag_rows(fine, fine_tags, lane_ref[0:1, :fine_lanes], lane_ref[1:2, :fine_lanes], fine_lanes)
    tag_own[: fine.down, :fine_lanes] = top.astype(jnp.bfloat16)
    low = tag_rows(coarse, coarse_tags, lane_ref[0:1, fine_lanes:], lane_ref[1:2, fine_lanes:], coarse_lanes)
    tag_own[: coarse.down, fine_lanes:] = low.astype(jnp.bfloat16)
    pl.semaphore_wait(barrier, peers)
    gather.begin()

    def tag_copy(side):
        dy, dx = AROUND[side]
        return around.copy(tag_own, tag_wide.at[side], tag_send.at[side], tag_recv.at[side], dy, dx)

    for side, (dy, dx) in enumerate(AROUND):
        around.when_there(-dy, lambda side=side: tag_copy(side).start())

    fetch.wait()
    normed = normalize(tokens[...], fine_gain[...])
    arranged = pick(index_ref[: fine.quads * ROWS, 0:1], normed)
    own[...] = arranged
    halo = Halo(around, fine, own, wide, send1, recv1)
    halo.start()
    for q in range(fine.quads):
        spot = fine.spot(*divmod(q, fine.across))
        wide[pl.ds(spot * ROWS, ROWS), :] = arranged[q * ROWS : (q + 1) * ROWS]

    parts = split_table((fine_table, coarse_table), padded)
    fine_bias[...] = jnp.zeros_like(fine_bias)
    coarse_bias[...] = jnp.zeros_like(coarse_bias)
    chunk = 4 * QUAD // 4
    for first in range(0, 4 * QUAD, chunk):
        fill_bias(parts, number_ref, (fine_bias, coarse_bias), first, first + chunk)
        gather.step()

    for side, (dy, dx) in enumerate(AROUND):
        around.when_there(dy, lambda side=side: tag_copy(side).wait_recv())
    tags = [tag_wide[side].astype(jnp.float32) for side in range(len(AROUND))] + [tag_own[...].astype(jnp.float32)]
    fill_masks(fine, tags, 0, fine_masks)
    fill_masks(coarse, tags, fine_lanes, coarse_masks)

    gather.ready(0)
    half = width // lvls
    for lvl in range(lvls):
        part = jnp.dot(turned(own, slice(None), block_of, lons), flat(f0[lvl, 0]), preferred_element_type=jnp.float32)
        query[:, lvl * half : (lvl + 1) * half] = (part * scale).astype(jnp.bfloat16)
    halo.finish()
    for member, target in ((1, keys), (2, values)):
        gather.ready(member)

        @pl.loop(0, fine.windows // fine.columns)
        def _(band):
            count = fine.columns * WINDOW
            rows = pl.ds(pl.multiple_of(band * count, count), count)
            x = turned(wide, rows, block_of, lons)
            for lvl in range(lvls):
                part = jnp.dot(x, flat(f0[lvl, member]), preferred_element_type=jnp.float32)
                target[rows, lvl * half : (lvl + 1) * half] = part.astype(jnp.bfloat16)

    per_row = fine.across
    for first in range(0, fine.quads, per_row):
        @pl.loop(first, first + per_row)
        def _(q):
            for group in range(width // LANES):
                attend(fine, q, group, query, keys, values, fine_bias, fine_masks, mixed, size)
        gather.step()

    own_mixed = pick(index_ref[: fine.own, 1:2], mixed[...])
    gather.ready(3)
    update = None
    for lvl in range(lvls):
        term = lax.dot_general(
            own_mixed[:, lvl * half : (lvl + 1) * half], flat(f1[lvl, 0]), NT, preferred_element_type=jnp.float32
        )
        update = term if update is None else update + term

    def put_fine(cols, value):
        fine_value[:, cols] = (tokens[:, cols].astype(jnp.float32) + value).astype(jnp.bfloat16)

    turn_back(update, block_of, lons, put_fine)
    publish = pltpu.make_async_copy(fine_value, fine_ref, local.at[1])
    publish.start()

    count = coarse.quads * ROWS
    stacked = pick(index_ref[: 4 * count, 2:3], fine_value[...]).astype(jnp.float32)
    members = [stacked[m * count : (m + 1) * count] for m in range(4)]
    mean = sum(jnp.sum(m, axis=-1, keepdims=True) for m in members) / (4 * width)
    centers = [m - mean for m in members]
    spread = sum(jnp.sum(c * c, axis=-1, keepdims=True) for c in centers) / (4 * width)
    factor = lax.rsqrt(spread + EPSILON)
    normed = jnp.concatenate(
        [(centers[m] * factor * merge_gain[:, m * width : (m + 1) * width]).astype(jnp.bfloat16) for m in range(4)],
        axis=1,
    )
    merged = None
    share = 4 * width // lvls
    for u in range(4, 8):
        gather.ready(u)
        _, _, _, col, cols = units[u]
        for lvl in range(lvls):
            start = lvl * share + col
            term = lax.dot_general(
                normed[:, start : start + cols], flat(f2[lvl, 0, :, :, col : col + cols]), NT,
                preferred_element_type=jnp.float32,
            )
            merged = term if merged is None else merged + term

    def put_coarse(cols, value):
        two_in[:, cols] = value.astype(jnp.bfloat16)

    turn_back(merged, block_of, lons, put_coarse)
    two_own[...] = normalize(two_in[...], coarse_gain[...])
    halo_two = Halo(around, coarse, two_own, two_wide, send2, recv2)
    halo_two.start()
    for q in range(coarse.quads):
        spot = coarse.spot(*divmod(q, coarse.across))
        two_wide[pl.ds(spot * ROWS, ROWS), :] = two_own[q * ROWS : (q + 1) * ROWS, :]
    gather.step()
    halo_two.finish()

    share = wide_two // lvls
    inner = [u for u in range(len(units)) if units[u][0] == 3]
    for u in inner:
        gather.ready(u)
        _, _, _, col, cols = units[u]
        for lvl in range(lvls):
            start = lvl * share + col
            part = jnp.dot(
                turned(two_own, slice(None), block_of, lons), flat(f3[lvl, 0, :, :, col : col + cols]),
                preferred_element_type=jnp.float32,
            )
            two_query[:, start : start + cols] = (part * scale).astype(jnp.bfloat16)
            weight = jnp.concatenate([flat(f3[lvl, k, :, :, col : col + cols]) for k in (1, 2)], axis=1)
            part = jnp.dot(
                turned(two_wide, slice(None), block_of, lons), weight, preferred_element_type=jnp.float32
            ).astype(jnp.bfloat16)
            two_keys[:, start : start + cols] = part[:, :cols]
            two_values[:, start : start + cols] = part[:, cols:]

        @pl.loop(0, coarse.quads)
        def _(q):
            for lvl in range(lvls):
                group = (lvl * share + col) // LANES
                attend(coarse, q, group, two_query, two_keys, two_values, coarse_bias, coarse_masks, two_mixed, size)

    update = None
    for u in [u for u in range(len(units)) if units[u][0] == 4]:
        gather.ready(u)
        _, _, _, col, cols = units[u]
        for lvl in range(lvls):
            start = lvl * share + col
            term = lax.dot_general(
                two_mixed[:, start : start + cols], flat(f4[lvl, 0, :, :, col : col + cols]), NT,
                preferred_element_type=jnp.float32,
            )
            update = term if update is None else update + term

    def put_out(cols, value):
        two_value[:, cols] = (two_in[:, cols].astype(jnp.float32) + value).astype(jnp.bfloat16)

    turn_back(update, block_of, lons, put_out)
    pitch = up_to(coarse.lon_len, 16)
    result = pick(index_ref[: coarse.lat_len * pitch, 3:4], two_value[...])
    for r in range(coarse.lat_len):
        coarse_ref[r] = result[r * pitch : r * pitch + coarse.lon_len]

    publish.wait()
    gather.end()
    for side, (dy, dx) in enumerate(AROUND):
        around.when_there(-dy, lambda side=side: tag_copy(side).wait_send())
    halo.drain()
    halo_two.drain()


def level_scratch(plan, features, heads):
    rows, all_rows = plan.quads * ROWS, plan.windows * WINDOW
    return [
        pltpu.VMEM((rows, features), jnp.bfloat16),
        pltpu.VMEM((all_rows, features), jnp.bfloat16),
        pltpu.VMEM((rows, features), jnp.bfloat16),
        pltpu.VMEM((all_rows, features), jnp.bfloat16),
        pltpu.VMEM((all_rows, features), jnp.bfloat16),
        pltpu.VMEM((rows, features), jnp.bfloat16),
        pltpu.VMEM((heads, WINDOW, LANES), jnp.float32),
        pltpu.VMEM((plan.quads, ROWS, LANES), jnp.float32),
    ]


def shards(
    tokens, fine_tags, coarse_tags, fine_gain, fine_inward, fine_outward, fine_table, merge_gain,
    merge_weight, coarse_gain, coarse_inward, coarse_outward, coarse_table,
):
    _, lat_len, lon_len, width = tokens.shape
    fine, coarse = Plan(lat_len, lon_len), Plan(lat_len // 2, lon_len // 2)
    weights = [fine_inward, fine_outward[None], merge_weight[None], coarse_inward, coarse_outward[None]]
    grps, lats, lons, lvls = (lax.axis_size(a) for a in ("grp", "lat", "lon", "lvl"))
    split = grps == 2 and lats == 2 and all(w.shape[1] % LANES == 0 for w in weights)
    units = weight_units(weights)
    wide_two = coarse_inward.shape[1] * lons
    heads, heads_two = fine_table.shape[0], coarse_table.shape[0]
    pitch = up_to(coarse.lon_len, 16)

    columns = [fine.natural(), fine.back(fine.lon_len), patches(fine, coarse), coarse.back(pitch)]
    index = np.full((max(len(c) for c in columns), len(columns)), -1, np.int32)
    for n, column in enumerate(columns):
        index[: len(column), n] = column
    lane = np.concatenate([np.stack(p.lanes()) for p in (fine, coarse)], axis=1).astype(np.int32)

    dma = pltpu.SemaphoreType.DMA
    bf16 = jnp.bfloat16
    sides = len(AROUND)
    fine_out, coarse_out = pl.pallas_call(
        functools.partial(kernel, fine, coarse, units, split),
        out_shape=[
            jax.ShapeDtypeStruct((fine.own, width), bf16),
            jax.ShapeDtypeStruct((coarse.lat_len, coarse.lon_len, wide_two), bf16),
        ],
        in_specs=[ANY] + [VMEM] * 10 + [ANY] * 5,
        out_specs=[ANY, VMEM],
        scratch_shapes=[pltpu.VMEM((fine.own, width), bf16)]
        + level_scratch(fine, width, heads)
        + [pltpu.VMEM((fine.own, width), bf16)]
        + level_scratch(coarse, wide_two, heads_two)
        + [pltpu.VMEM((coarse.quads * ROWS, wide_two), bf16)] * 2
        + [
            pltpu.VMEM((heads + heads_two, up_to(fine_table.shape[1], LANES)), jnp.float32),
            pltpu.VMEM((16, lane.shape[1]), bf16),
            pltpu.VMEM((sides, 16, lane.shape[1]), bf16),
        ]
        + [pltpu.VMEM((lvls, w.shape[0], lons, w.shape[1], w.shape[2]), bf16) for w in weights]
        + [dma((2,)), dma((sides,)), dma((sides,))]
        + [dma((len(fine.halo),))] * 2
        + [dma((len(coarse.halo),))] * 2
        + gather_scratch(units, split),
        compiler_params=pltpu.CompilerParams(collective_id=1, has_side_effects=True, vmem_limit_bytes=LIMIT),
        name="levels",
    )(
        tokens.reshape(fine.own, width), fine_tags.reshape(lat_len, 1, lon_len),
        coarse_tags.reshape(coarse.lat_len, 1, coarse.lon_len), fine_gain[None], merge_gain[None], coarse_gain[None],
        fine_table, coarse_table, index, offset_numbers(), lane, *weights,
    )
    return fine_out.reshape(tokens.shape), coarse_out[None]


def solution(mesh):
    placed = (
        P(("grp", "lvl"), "lat", "lon", None),
        P(("grp", "lvl"), "lat", "lon"),
        P(("grp", "lvl"), "lat", "lon"),
        P(),
        P(None, "lon", "lvl"),
        P("lon", "lvl"),
        P(),
        P(),
        P("lon", "lvl"),
        P(),
        P(None, "lon", "lvl"),
        P("lon", "lvl"),
        P(),
    )
    return jax.shard_map(
        shards,
        mesh=mesh,
        in_specs=placed,
        out_specs=(P(("grp", "lvl"), "lat", "lon", None), P(("grp", "lvl"), "lat", "lon", None)),
        check_vma=False,
    )
```

time: 139 us -> 104 us (0.75)
  Pallas kernels: 125 us -> 101 us
  other arithmetic: 8.45 us -> 0 us
  local copies, waits for them, and re-layouts: 4.51 us -> 2.41 us
    pallas_call x2 -> x1, Pallas kernels: 125 us -> 101 us  [shards(): pl.pallas_call(functools.partial(kernel, fine, coarse, units, split), out...]
    concatenate x6 -> x0, other arithmetic: 4.78 us -> none  [the longest x4 3.53 us: shards(): jnp.concatenate([tokens[0], jnp.broadcast_to(fine_tags[0, :, :, None], (l...]
    convert_element_type x5 -> x0, other arithmetic: 3.67 us -> none  [the longest x2 1.49 us: table_parts(): terms.append(term.astype(jnp.bfloat16))]
where the time goes in v1:
time: 104 us
  Pallas kernels  101 us (97%)
  local copies, waits for them, and re-layouts  2.41 us (2%)
    pallas_call x1, Pallas kernels, shards(): pl.pallas_call(functools.partial(kernel, fine, coarse, units, split), out...  101 us
    unnamed x4, local copies, waits for them, and re-layouts  2.41 us

profile of v1, /device:TPU:0, one launch (start us, length us, event | category | flops | bytes accessed | tf_op | source)
XLA Modules:
  0.0 103.6 jit_solution(17858289380753530623)
XLA Ops:
  0.6 100.6 %levels.1 = (bf16[288,512]{1,0:T(8,128)(2,1)}, bf16[6,12,1024]{2,1,0:T(8,128)(2,1)}) custom-call(bf16[288,512]{1,0:T(8,128)(2,1)} %bitcast.12, s32[12,1,24]{2,1,0:T(1,128)} %bitcast.18, s32[6,1,12]{2,1,0:T(1,128)} %bitcast.20, f32[1,512]{1,0:T(1,128)} %bitcast.21, f32[1,2048]{1,0:T(1,128)} %bitcast.17, f32[1,1024]{1,0:T(1,128)} %bitcast.19, ...), custom_call_target="tpu_custom_call" | custom-call | tf_op jit(solution)/shard_map/levels/pallas_call | solution.py:688
  101.2 0.0 copy-start
  101.2 1.7 %copy.20 = bf16[1,12,24,512]{3,2,1,0:T(8,128)(2,1)} copy(bf16[1,12,24,512]{3,2,1,0:T(8,128)(2,1)} %bitcast.13) | data formatting | bytes 589824
  103.0 0.0 copy-done
  103.0 0.7 copy.21
Async XLA Ops:
  101.2 1.7 %copy-start = (bf16[6,12,1024]{2,1,0:T(8,128)(2,1)S(1)}, bf16[6,12,1024]{2,1,0:T(8,128)(2,1)}, u32[]{:S(2)}) copy-start(bf16[6,12,1024]{2,1,0:T(8,128)(2,1)} %get-tuple-element.5) | copy-start | bytes 442372

commit v2 on v1

--- a/solution.py
+++ b/solution.py
@@ -15,6 +15,7 @@
 HALF_LON = WIN_LON // 2
 QUAD = HALF_LAT * HALF_LON
 ROWS = -(-QUAD // 16) * 16
+SENT = -(-QUAD // 8) * 8
 WINDOW = 4 * ROWS
 EPSILON = 1e-05
 LANES = 128
@@ -154,19 +155,18 @@
     def copy(self, n):
         side, r, c, q = self.plan.halo[n]
         return self.around.copy(
-            self.own.at[pl.ds(q * ROWS, ROWS)], self.wide.at[pl.ds(self.plan.spot(r, c) * ROWS, ROWS)],
+            self.own.at[pl.ds(q * ROWS, SENT)], self.wide.at[pl.ds(self.plan.spot(r, c) * ROWS, SENT)],
             self.send.at[n], self.recv.at[n], *AROUND[side],
         )
 
+    def clear(self):
+        for _, r, c, _ in self.plan.halo:
+            rows = pl.ds(self.plan.spot(r, c) * ROWS, ROWS)
+            self.wide[rows, :] = jnp.zeros((ROWS, self.wide.shape[1]), self.wide.dtype)
+
     def start(self):
-        for n, (side, r, c, _) in enumerate(self.plan.halo):
-            dy = AROUND[side][0]
-            self.around.when_there(-dy, lambda n=n: self.copy(n).start())
-            if dy:
-                def clear(r=r, c=c):
-                    rows = pl.ds(self.plan.spot(r, c) * ROWS, ROWS)
-                    self.wide[rows, :] = jnp.zeros((ROWS, self.wide.shape[1]), self.wide.dtype)
-                pl.when(jnp.logical_not(self.around.there(dy)))(clear)
+        for n, (side, *_) in enumerate(self.plan.halo):
+            self.around.when_there(-AROUND[side][0], lambda n=n: self.copy(n).start())
 
     def finish(self):
         for n, (side, *_) in enumerate(self.plan.halo):
@@ -368,7 +368,9 @@
             r = q * HALF_LAT + k
             row = jnp.where(place == k, spread[r : r + 1, :], row)
         rows.append(row)
-    return jnp.concatenate(rows, axis=0)
+    return jnp.concatenate(
+        [row[:, c * LANES : (c + 1) * LANES] for row in rows for c in range(plan.across)], axis=0
+    )
 
 
 def fill_masks(plan, tags, offset, masks):
@@ -380,8 +382,8 @@
         dy = -1 if r < 0 else int(r >= plan.down)
         dx = -1 if c < 0 else int(c >= plan.across)
         side = AROUND.index((dy, dx)) if dy or dx else len(AROUND)
-        r, c = r % plan.down, c % plan.across
-        return tags[side][r : r + 1, offset + c * LANES : offset + (c + 1) * LANES]
+        row = offset + r % plan.down * plan.across + c % plan.across
+        return tags[side][row : row + 1]
 
     for q in range(plan.quads):
         r, c = divmod(q, plan.across)
@@ -422,35 +424,39 @@
             start += bias.shape[0]
 
 
-def attend(plan, q, group, query, keys, values, bias_ref, masks, mixed, size):
+def attend(plan, spots, query, keys, values, bias_ref, masks, mixed, size):
     heads = LANES // size
-    r = lax.div(q, plan.across)
-    c = q - r * plan.across
-    window = lax.div(r + 1, 2) * plan.columns + lax.div(c + 1, 2)
-    place = lax.rem(r + 1, 2) * 2 + lax.rem(c + 1, 2)
-    rows = pl.ds(pl.multiple_of(q * ROWS, ROWS), ROWS)
-    others = pl.ds(pl.multiple_of(window * WINDOW, WINDOW), WINDOW)
-    inside = pl.ds(pl.multiple_of(place * ROWS, ROWS), ROWS)
-    cols = slice(group * LANES, (group + 1) * LANES)
     owner = lax.broadcasted_iota(jnp.int32, (ROWS, LANES), 1) // size
-    block = query[rows, cols]
-    stack = jnp.concatenate([jnp.where(owner == h, block, jnp.zeros_like(block)) for h in range(heads)], axis=0)
-    scores = lax.dot_general(stack, keys[others, cols], NT, preferred_element_type=jnp.float32)
-    mask = masks[q]
-    weights = []
-    for h in range(heads):
-        score = scores[h * ROWS : (h + 1) * ROWS] + bias_ref[group * heads + h, inside, :] + mask
+    ones = jnp.ones((WINDOW, LANES), jnp.bfloat16)
+    where, scores, weights, both = [], [], [], []
+    for q, group in spots:
+        r = lax.div(q, plan.across)
+        c = q - r * plan.across
+        window = lax.div(r + 1, 2) * plan.columns + lax.div(c + 1, 2)
+        place = lax.rem(r + 1, 2) * 2 + lax.rem(c + 1, 2)
+        where.append((
+            q, group, pl.ds(pl.multiple_of(q * ROWS, ROWS), ROWS), pl.ds(pl.multiple_of(window * WINDOW, WINDOW), WINDOW),
+            pl.ds(pl.multiple_of(place * ROWS, ROWS), ROWS), slice(group * LANES, (group + 1) * LANES),
+        ))
+    for q, group, rows, others, inside, cols in where:
+        block = query[rows, cols]
+        stack = jnp.concatenate([jnp.where(owner == h, block, jnp.zeros_like(block)) for h in range(heads)], axis=0)
+        scores.append(lax.dot_general(stack, keys[others, cols], NT, preferred_element_type=jnp.float32))
+    for (q, group, rows, others, inside, cols), score in zip(where, scores):
+        bias = bias_ref[group * heads : (group + 1) * heads, inside, :].reshape(heads * ROWS, LANES)
+        score = score + bias + jnp.concatenate([masks[q]] * heads, axis=0)
         weights.append(jnp.exp2(score - jnp.max(score, axis=-1, keepdims=True)).astype(jnp.bfloat16))
-    weights = jnp.concatenate(weights, axis=0)
-    ones = jnp.ones((WINDOW, LANES), jnp.bfloat16)
-    both = jnp.dot(weights, jnp.concatenate([values[others, cols], ones], axis=1), preferred_element_type=jnp.float32)
-    result = both[:ROWS]
-    blended, totals = result[:, :LANES], result[:, LANES:]
-    for h in range(1, heads):
-        result = both[h * ROWS : (h + 1) * ROWS]
-        blended = jnp.where(owner == h, result[:, :LANES], blended)
-        totals = jnp.where(owner == h, result[:, LANES:], totals)
-    mixed[rows, cols] = (blended / totals).astype(jnp.bfloat16)
+    for (q, group, rows, others, inside, cols), weight in zip(where, weights):
+        both.append(jnp.dot(
+            weight, jnp.concatenate([values[others, cols], ones], axis=1), preferred_element_type=jnp.float32
+        ))
+    for (q, group, rows, others, inside, cols), part in zip(where, both):
+        blended, totals = part[:ROWS, :LANES], part[:ROWS, LANES:]
+        for h in range(1, heads):
+            result = part[h * ROWS : (h + 1) * ROWS]
+            blended = jnp.where(owner == h, result[:, :LANES], blended)
+            totals = jnp.where(owner == h, result[:, LANES:], totals)
+        mixed[rows, cols] = (blended / totals).astype(jnp.bfloat16)
 
 
 def kernel(
@@ -471,16 +477,19 @@
     fetch = pltpu.make_async_copy(tokens_ref, tokens, local.at[0])
     fetch.start()
     tag_wide[...] = jnp.zeros_like(tag_wide)
+    halo = Halo(around, fine, own, wide, send1, recv1)
+    halo_two = Halo(around, coarse, two_own, two_wide, send2, recv2)
+    halo.clear()
+    halo_two.clear()
     barrier = pltpu.get_barrier_semaphore()
     peers = around.greet(barrier) + gather.greet(barrier)
 
     fine_lanes = fine.across * LANES
     coarse_lanes = coarse.across * LANES
-    tag_own[...] = jnp.zeros_like(tag_own)
     top = tag_rows(fine, fine_tags, lane_ref[0:1, :fine_lanes], lane_ref[1:2, :fine_lanes], fine_lanes)
-    tag_own[: fine.down, :fine_lanes] = top.astype(jnp.bfloat16)
+    spare = jnp.zeros((tag_own.shape[0] - fine.quads - coarse.quads, LANES), jnp.float32)
     low = tag_rows(coarse, coarse_tags, lane_ref[0:1, fine_lanes:], lane_ref[1:2, fine_lanes:], coarse_lanes)
-    tag_own[: coarse.down, fine_lanes:] = low.astype(jnp.bfloat16)
+    tag_own[...] = jnp.concatenate([top, low, spare], axis=0).astype(jnp.bfloat16)
     pl.semaphore_wait(barrier, peers)
     gather.begin()
 
@@ -495,7 +504,6 @@
     normed = normalize(tokens[...], fine_gain[...])
     arranged = pick(index_ref[: fine.quads * ROWS, 0:1], normed)
     own[...] = arranged
-    halo = Halo(around, fine, own, wide, send1, recv1)
     halo.start()
     for q in range(fine.quads):
         spot = fine.spot(*divmod(q, fine.across))
@@ -513,7 +521,7 @@
         around.when_there(dy, lambda side=side: tag_copy(side).wait_recv())
     tags = [tag_wide[side].astype(jnp.float32) for side in range(len(AROUND))] + [tag_own[...].astype(jnp.float32)]
     fill_masks(fine, tags, 0, fine_masks)
-    fill_masks(coarse, tags, fine_lanes, coarse_masks)
+    fill_masks(coarse, tags, fine.quads, coarse_masks)
 
     gather.ready(0)
     half = width // lvls
@@ -535,10 +543,12 @@
 
     per_row = fine.across
     for first in range(0, fine.quads, per_row):
-        @pl.loop(first, first + per_row)
+        @pl.loop(first, first + per_row, step=2)
         def _(q):
-            for group in range(width // LANES):
-                attend(fine, q, group, query, keys, values, fine_bias, fine_masks, mixed, size)
+            attend(
+                fine, [(q + i, group) for i in range(2) for group in range(width // LANES)], query, keys, values,
+                fine_bias, fine_masks, mixed, size,
+            )
         gather.step()
 
     own_mixed = pick(index_ref[: fine.own, 1:2], mixed[...])
@@ -586,7 +596,6 @@
 
     turn_back(merged, block_of, lons, put_coarse)
     two_own[...] = normalize(two_in[...], coarse_gain[...])
-    halo_two = Halo(around, coarse, two_own, two_wide, send2, recv2)
     halo_two.start()
     for q in range(coarse.quads):
         spot = coarse.spot(*divmod(q, coarse.across))
@@ -613,11 +622,10 @@
             two_keys[:, start : start + cols] = part[:, :cols]
             two_values[:, start : start + cols] = part[:, cols:]
 
-        @pl.loop(0, coarse.quads)
-        def _(q):
-            for lvl in range(lvls):
-                group = (lvl * share + col) // LANES
-                attend(coarse, q, group, two_query, two_keys, two_values, coarse_bias, coarse_masks, two_mixed, size)
+        attend(
+            coarse, [(q, (lvl * share + col) // LANES) for q in range(coarse.quads) for lvl in range(lvls)],
+            two_query, two_keys, two_values, coarse_bias, coarse_masks, two_mixed, size,
+        )
 
     update = None
     for u in [u for u in range(len(units)) if units[u][0] == 4]:
@@ -684,7 +692,7 @@
 
     dma = pltpu.SemaphoreType.DMA
     bf16 = jnp.bfloat16
-    sides = len(AROUND)
+    sides, tag_count = len(AROUND), up_to(fine.quads + coarse.quads, 16)
     fine_out, coarse_out = pl.pallas_call(
         functools.partial(kernel, fine, coarse, units, split),
         out_shape=[
@@ -700,8 +708,8 @@
         + [pltpu.VMEM((coarse.quads * ROWS, wide_two), bf16)] * 2
         + [
             pltpu.VMEM((heads + heads_two, up_to(fine_table.shape[1], LANES)), jnp.float32),
-            pltpu.VMEM((16, lane.shape[1]), bf16),
-            pltpu.VMEM((sides, 16, lane.shape[1]), bf16),
+            pltpu.VMEM((tag_count, LANES), bf16),
+            pltpu.VMEM((sides, tag_count, LANES), bf16),
         ]
         + [pltpu.VMEM((lvls, w.shape[0], lons, w.shape[1], w.shape[2]), bf16) for w in weights]
         + [dma((2,)), dma((sides,)), dma((sides,))]

time: 104 us -> 88.5 us (0.85); the launches traced: 104 us -> 86.9 us
  Pallas kernels: 101 us -> 83.8 us
    pallas_call x1, Pallas kernels: 101 us -> 83.8 us  [shards(): pl.pallas_call(functools.partial(kernel, fine, coarse, units, split), out...]
where the time goes in v2:
time: 88.5 us; the launch traced here: 86.9 us
  Pallas kernels  83.8 us (95%)
  local copies, waits for them, and re-layouts  2.41 us (3%)
    pallas_call x1, Pallas kernels, shards(): pl.pallas_call(functools.partial(kernel, fine, coarse, units, split), out...  83.8 us
    unnamed x4, local copies, waits for them, and re-layouts  2.41 us

profile of v2, /device:TPU:0, one launch (start us, length us, event | category | flops | bytes accessed | tf_op | source)
XLA Modules:
  0.0 86.9 jit_solution(13626813116952371230)
XLA Ops:
  0.6 83.8 %levels.1 = (bf16[288,512]{1,0:T(8,128)(2,1)}, bf16[6,12,1024]{2,1,0:T(8,128)(2,1)}) custom-call(bf16[288,512]{1,0:T(8,128)(2,1)} %bitcast.12, s32[12,1,24]{2,1,0:T(1,128)} %bitcast.18, s32[6,1,12]{2,1,0:T(1,128)} %bitcast.20, f32[1,512]{1,0:T(1,128)} %bitcast.21, f32[1,2048]{1,0:T(1,128)} %bitcast.17, f32[1,1024]{1,0:T(1,128)} %bitcast.19, ...), custom_call_target="tpu_custom_call" | custom-call | tf_op jit(solution)/shard_map/levels/pallas_call | solution.py:696
  84.5 0.0 copy-start
  84.5 1.7 %copy.20 = bf16[1,12,24,512]{3,2,1,0:T(8,128)(2,1)} copy(bf16[1,12,24,512]{3,2,1,0:T(8,128)(2,1)} %bitcast.13) | data formatting | bytes 589824
  86.2 0.0 copy-done
  86.2 0.7 copy.21
Async XLA Ops:
  84.5 1.7 %copy-start = (bf16[6,12,1024]{2,1,0:T(8,128)(2,1)S(1)}, bf16[6,12,1024]{2,1,0:T(8,128)(2,1)}, u32[]{:S(2)}) copy-start(bf16[6,12,1024]{2,1,0:T(8,128)(2,1)} %get-tuple-element.5) | copy-start | bytes 442372

commit v3 on v2

--- a/solution.py
+++ b/solution.py
@@ -23,10 +23,18 @@
 MESH = pl.DeviceIdType.MESH
 VMEM = pl.BlockSpec(memory_space=pltpu.VMEM)
 ANY = pl.BlockSpec(memory_space=pl.ANY)
+HBM = pl.BlockSpec(memory_space=pltpu.HBM)
 LIMIT = 60 * 1024 * 1024
 NT = (((1,), (1,)), ((), ()))
 AROUND = ((0, -1), (0, 1), (-1, 0), (1, 0), (-1, -1), (-1, 1), (1, -1), (1, 1))
-AHEAD = 2
+AHEAD = 3
+LAG = 2
+RELAYED = 3
+ORDER = (2, 1, 3)
+MERGE = 256
+LAST = 256
+SMALL = 10
+FIRST = (32, 48)
 
 
 def up_to(count, step):
@@ -182,10 +190,10 @@
         self.shards, self.fulls, self.units, self.split, self.sems = shards, fulls, units, split, sems
         self.index = {a: lax.axis_index(a) for a in ("grp", "lat", "lon", "lvl")}
         self.size = {a: lax.axis_size(a) for a in ("grp", "lat", "lon", "lvl")}
-        self.halves = range(2 if split else 1)
-        self.ways = [(s, half) for s in range(1, self.size["lon"]) for half in self.halves]
-        self.now = 0
-        self.steps = len(units) + (2 if split else 0)
+        self.slots = range(1, self.size["lon"])
+        self.plane = ("lat", "grp")
+        self.line = split and self.size["lon"] == 4
+        self.now = self.arrived = self.forwarded = self.shared = 0
 
     def at(self, axis, step):
         return {axis: lax.rem(self.index[axis] + step + self.size[axis], self.size[axis])}
@@ -204,20 +212,12 @@
     def rows(self, u):
         return self.shards[self.units[u][0]].shape[1]
 
-    def axes(self, half):
-        return ("lat", "grp") if half == 0 else ("grp", "lat")
-
-    def piece(self, u, half):
+    def piece(self, u, other=None):
         if not self.split:
             return 0, self.rows(u)
-        size = self.rows(u) // 8
-        first, second = self.axes(half)
-        order = self.index[second] * 2 + self.index[first]
-        return pl.multiple_of((half * 4 + order) * size, 16), size
-
-    def pair(self, u, half):
-        size = self.rows(u) // 8
-        return pl.multiple_of((half * 4 + self.index[self.axes(half)[1]] * 2) * size, 16), 2 * size
+        size = self.rows(u) // 4
+        lat, grp = [1 - self.index[a] if a == other else self.index[a] for a in self.plane]
+        return pl.multiple_of((lat * 2 + grp) * size, 16), size
 
     def held(self, u, start, size):
         m, k, depth, col, cols = self.units[u]
@@ -246,92 +246,134 @@
             self.held(u, 0, self.rows(u)), self.slot(u, slot, 0, self.rows(u)), self.sems[0].at[u]
         )
 
-    def lon_copy(self, u, s, half):
-        start, size = self.piece(u, half)
+    def lon_copy(self, u, s):
+        start, size = self.piece(u)
         slot = s if self.split else self.index["lon"]
         return self.remote(
-            self.held(u, start, size), self.slot(u, slot, start, size), 0, (u, s - 1, half), self.at("lon", -s)
+            self.held(u, start, size), self.slot(u, slot, start, size), 0, (u, s - 1), self.at("lon", -s)
         )
 
-    def one_copy(self, u, half):
-        block = self.block(u, 1, self.size["lon"] - 1, *self.piece(u, half))
-        return self.remote(block, block, 1, (u, half), self.at(self.axes(half)[0], 1))
-
-    def two_copy(self, u, half):
-        block = self.block(u, 1, self.size["lon"] - 1, *self.pair(u, half))
-        return self.remote(block, block, 2, (u, half), self.at(self.axes(half)[1], 1))
+    def near_copy(self, u, n):
+        block = self.block(u, 1, self.size["lon"] - 1, *self.piece(u))
+        return self.remote(block, block, 1, (u, n), self.at(self.plane[n], 1))
+
+    def far_copy(self, u, n):
+        start, size = self.piece(u, self.plane[n])
+        cut = size * FIRST[u % len(FIRST)] // 64 // 16 * 16
+        start, size = (start, cut) if n == 0 else (pl.multiple_of(start + cut, 16), size - cut)
+        block = self.block(u, 1, self.size["lon"] - 1, start, size)
+        return self.remote(block, block, 2, (u, n), self.at(self.plane[1 - n], 1))
 
     def lvl_copy(self, u):
         block = self.block(u, 0, self.size["lon"], 0, self.rows(u))
         return self.remote(block, block, 3, (u,), self.at("lvl", 1))
 
+    def relayed(self, u):
+        return self.line and RELAYED <= u < len(self.units)
+
+    def direct(self, u, s, action):
+        if s == 2 or not self.relayed(u):
+            action()
+        else:
+            pl.when(self.index["lon"] > 0 if s == 1 else self.index["lon"] < 3)(action)
+
+    def relays(self, u, action):
+        for lon, slot, step in ((2, 1, 1), (1, 3, -1)) if self.relayed(u) else ():
+            def act(slot=slot, step=step):
+                place = self.piece(u)
+                action(pltpu.make_async_remote_copy(
+                    src_ref=self.slot(u, 2, *place), dst_ref=self.slot(u, slot, *place),
+                    send_sem=self.sems[9].at[u], recv_sem=self.sems[2].at[u, slot - 1],
+                    device_id=self.at("lon", step), device_id_type=MESH,
+                ))
+            pl.when(self.index["lon"] == lon)(act)
+
+    def relay(self, u):
+        if self.relayed(u):
+            self.lon_copy(u, 2).wait_recv()
+            self.relays(u, lambda copy: copy.start())
+
     def issue(self, u):
         if u < len(self.units):
-            for s, half in self.ways:
-                self.lon_copy(u, s, half).start()
+            for s in ORDER if self.line else self.slots:
+                self.direct(u, s, lambda s=s: self.lon_copy(u, s).start())
             self.own_copy(u).start()
 
     def begin(self):
         for u in range(AHEAD):
             self.issue(u)
 
-    def step(self):
-        k, count = self.now, len(self.units)
-        self.now += 1
-        if k < count:
-            for half in self.halves:
-                for s in range(1, self.size["lon"]):
-                    self.lon_copy(k, s, half).wait_recv()
-                if self.split:
-                    self.one_copy(k, half).start()
-            self.issue(k + AHEAD)
-        if self.split and 0 <= k - 1 < count:
-            for half in self.halves:
-                self.one_copy(k - 1, half).wait_recv()
-                self.two_copy(k - 1, half).start()
-        done = k - 2 if self.split else k
-        if 0 <= done < count:
-            if self.split:
-                for half in self.halves:
-                    self.two_copy(done, half).wait_recv()
-            self.own_copy(done).wait()
-            self.lvl_copy(done).start()
-
-    def ready(self, *wanted):
-        for u in wanted:
-            while self.now <= u + (2 if self.split else 0):
-                self.step()
-            self.lvl_copy(u).wait_recv()
+    def arrive(self):
+        u = self.arrived
+        self.arrived += 1
+        for s in self.slots:
+            if s != 2 or not self.relayed(u):
+                self.lon_copy(u, s).wait_recv()
+        if self.split:
+            for n in range(2):
+                self.near_copy(u, n).start()
+        self.issue(u + AHEAD)
+
+    def forward(self):
+        u = self.forwarded
+        self.forwarded += 1
+        if self.split:
+            for n in range(2):
+                self.near_copy(u, n).wait_recv()
+                self.far_copy(u, n).start()
+
+    def share(self):
+        u = self.shared
+        self.shared += 1
+        if self.split:
+            for n in range(2):
+                self.far_copy(u, n).wait_recv()
+        self.own_copy(u).wait()
+        self.lvl_copy(u).start()
+
+    def step(self, times=1):
+        for _ in range(times):
+            k, count = self.now, len(self.units)
+            self.now += 1
+            if k < count:
+                self.arrive()
+            if 0 <= k - LAG < count:
+                self.forward()
+            if 0 <= k - 2 * LAG < count:
+                self.share()
+            self.relay(k + 1)
+
+    def ready(self, u):
+        while self.shared <= u:
+            self.step()
+        self.lvl_copy(u).wait_recv()
 
     def end(self):
         for u in range(len(self.units)):
             self.lvl_copy(u).wait_send()
-            for s, half in self.ways:
-                self.lon_copy(u, s, half).wait_send()
+            for s in self.slots:
+                self.direct(u, s, lambda s=s: self.lon_copy(u, s).wait_send())
+            self.relays(u, lambda copy: copy.wait_send())
             if self.split:
-                for half in self.halves:
-                    self.one_copy(u, half).wait_send()
-                    self.two_copy(u, half).wait_send()
+                for n in range(2):
+                    self.near_copy(u, n).wait_send()
+                    self.far_copy(u, n).wait_send()
 
 
 def weight_units(shards):
     fine_inward, fine_outward, merge, coarse_inward, coarse_outward = [s.shape for s in shards]
     units = [(0, k, 1, 0, fine_inward[2]) for k in range(3)]
     units.append((1, 0, 1, 0, fine_outward[2]))
-    units += [(2, 0, 1, c, merge[2] // 4) for c in range(0, merge[2], merge[2] // 4)]
+    units += [(2, 0, 1, c, MERGE) for c in range(0, merge[2], MERGE)]
     units += [(3, 0, 3, c, LANES) for c in range(0, coarse_inward[2], LANES)]
-    half = coarse_outward[2] // 2
-    units += [(4, 0, 1, c, half) for c in (0, half)]
+    units += [(4, 0, 1, c, LAST) for c in range(0, coarse_outward[2], LAST)]
     return units
 
 
-def gather_scratch(units, split):
+def gather_scratch(units):
     count, lons = len(units), lax.axis_size("lon")
-    halves = 2 if split else 1
     dma = pltpu.SemaphoreType.DMA
-    return (
-        [dma((count,))] + [dma((count, lons - 1, halves))] * 2 + [dma((count, halves))] * 4 + [dma((count,))] * 2
-    )
+    return [dma((count,))] + [dma((count, lons - 1))] * 2 + [dma((count, 2))] * 4 + [dma((count,))] * 3
 
 
 def flat(block):
@@ -460,9 +502,15 @@
 
 
 def kernel(
-    fine, coarse, units, split, tokens_ref, fine_tags, coarse_tags, fine_gain, merge_gain, coarse_gain, fine_table,
-    coarse_table, index_ref, number_ref, lane_ref, s0, s1, s2, s3, s4, fine_ref, coarse_ref,
-    tokens, own, wide, query, keys, values, mixed, fine_bias, fine_masks, fine_value,
+    fine, coarse, units, split, tokens_ref, *refs,
+):
+    run(fine, coarse, units, split, tokens_ref, refs[:SMALL], *refs[SMALL:])
+
+
+def run(
+    fine, coarse, units, split, tokens_ref, small, s0, s1, s2, s3, s4, fine_ref, coarse_ref,
+    fine_tags, coarse_tags, lane_ref, fine_gain, index_ref, fine_table, coarse_table, number_ref, merge_gain,
+    coarse_gain, tokens, own, wide, query, keys, values, mixed, fine_bias, fine_masks, fine_value,
     two_own, two_wide, two_query, two_keys, two_values, two_mixed, coarse_bias, coarse_masks, two_in, two_value,
     padded, tag_own, tag_wide, f0, f1, f2, f3, f4, local, tag_send, tag_recv, send1, recv1, send2, recv2, *sems,
 ):
@@ -474,8 +522,6 @@
     lons, lvls = lax.axis_size("lon"), lax.axis_size("lvl")
     gather = Gather((s0, s1, s2, s3, s4), (f0, f1, f2, f3, f4), units, split, sems)
     block_of = gather.block_of
-    fetch = pltpu.make_async_copy(tokens_ref, tokens, local.at[0])
-    fetch.start()
     tag_wide[...] = jnp.zeros_like(tag_wide)
     halo = Halo(around, fine, own, wide, send1, recv1)
     halo_two = Halo(around, coarse, two_own, two_wide, send2, recv2)
@@ -483,15 +529,27 @@
     halo_two.clear()
     barrier = pltpu.get_barrier_semaphore()
     peers = around.greet(barrier) + gather.greet(barrier)
-
+    brought = (
+        fine_tags, coarse_tags, lane_ref, fine_gain, index_ref, fine_table, coarse_table, number_ref, merge_gain,
+        coarse_gain,
+    )
+    fetches = [pltpu.make_async_copy(src, dst, local.at[2 + n]) for n, (src, dst) in enumerate(zip(small, brought))]
+    for fetch in fetches[:3]:
+        fetch.start()
+    fetch = pltpu.make_async_copy(tokens_ref, tokens, local.at[0])
+    fetch.start()
+    for other in fetches[3:]:
+        other.start()
+    pl.semaphore_wait(barrier, peers)
+    gather.begin()
+    for other in fetches[:3]:
+        other.wait()
     fine_lanes = fine.across * LANES
     coarse_lanes = coarse.across * LANES
     top = tag_rows(fine, fine_tags, lane_ref[0:1, :fine_lanes], lane_ref[1:2, :fine_lanes], fine_lanes)
     spare = jnp.zeros((tag_own.shape[0] - fine.quads - coarse.quads, LANES), jnp.float32)
     low = tag_rows(coarse, coarse_tags, lane_ref[0:1, fine_lanes:], lane_ref[1:2, fine_lanes:], coarse_lanes)
     tag_own[...] = jnp.concatenate([top, low, spare], axis=0).astype(jnp.bfloat16)
-    pl.semaphore_wait(barrier, peers)
-    gather.begin()
 
     def tag_copy(side):
         dy, dx = AROUND[side]
@@ -501,6 +559,8 @@
         around.when_there(-dy, lambda side=side: tag_copy(side).start())
 
     fetch.wait()
+    fetches[3].wait()
+    fetches[4].wait()
     normed = normalize(tokens[...], fine_gain[...])
     arranged = pick(index_ref[: fine.quads * ROWS, 0:1], normed)
     own[...] = arranged
@@ -509,13 +569,16 @@
         spot = fine.spot(*divmod(q, fine.across))
         wide[pl.ds(spot * ROWS, ROWS), :] = arranged[q * ROWS : (q + 1) * ROWS]
 
+    for other in fetches[5:]:
+        other.wait()
     parts = split_table((fine_table, coarse_table), padded)
     fine_bias[...] = jnp.zeros_like(fine_bias)
     coarse_bias[...] = jnp.zeros_like(coarse_bias)
-    chunk = 4 * QUAD // 4
+    chunk = 4 * QUAD // 6
     for first in range(0, 4 * QUAD, chunk):
         fill_bias(parts, number_ref, (fine_bias, coarse_bias), first, first + chunk)
-        gather.step()
+        if first:
+            gather.step()
 
     for side, (dy, dx) in enumerate(AROUND):
         around.when_there(dy, lambda side=side: tag_copy(side).wait_recv())
@@ -580,7 +643,7 @@
     )
     merged = None
     share = 4 * width // lvls
-    for u in range(4, 8):
+    for u in [u for u in range(len(units)) if units[u][0] == 2]:
         gather.ready(u)
         _, _, _, col, cols = units[u]
         for lvl in range(lvls):
@@ -600,7 +663,7 @@
     for q in range(coarse.quads):
         spot = coarse.spot(*divmod(q, coarse.across))
         two_wide[pl.ds(spot * ROWS, ROWS), :] = two_own[q * ROWS : (q + 1) * ROWS, :]
-    gather.step()
+    gather.step(2)
     halo_two.finish()
 
     share = wide_two // lvls
@@ -690,6 +753,10 @@
         index[: len(column), n] = column
     lane = np.concatenate([np.stack(p.lanes()) for p in (fine, coarse)], axis=1).astype(np.int32)
 
+    small = [
+        fine_tags.reshape(lat_len, 1, lon_len), coarse_tags.reshape(coarse.lat_len, 1, coarse.lon_len), lane,
+        fine_gain[None], index, fine_table, coarse_table, offset_numbers(), merge_gain[None], coarse_gain[None],
+    ]
     dma = pltpu.SemaphoreType.DMA
     bf16 = jnp.bfloat16
     sides, tag_count = len(AROUND), up_to(fine.quads + coarse.quads, 16)
@@ -699,9 +766,10 @@
             jax.ShapeDtypeStruct((fine.own, width), bf16),
             jax.ShapeDtypeStruct((coarse.lat_len, coarse.lon_len, wide_two), bf16),
         ],
-        in_specs=[ANY] + [VMEM] * 10 + [ANY] * 5,
+        in_specs=[HBM] * (1 + SMALL + len(weights)),
         out_specs=[ANY, VMEM],
-        scratch_shapes=[pltpu.VMEM((fine.own, width), bf16)]
+        scratch_shapes=[pltpu.VMEM(x.shape, x.dtype) for x in small]
+        + [pltpu.VMEM((fine.own, width), bf16)]
         + level_scratch(fine, width, heads)
         + [pltpu.VMEM((fine.own, width), bf16)]
         + level_scratch(coarse, wide_two, heads_two)
@@ -712,16 +780,14 @@
             pltpu.VMEM((sides, tag_count, LANES), bf16),
         ]
         + [pltpu.VMEM((lvls, w.shape[0], lons, w.shape[1], w.shape[2]), bf16) for w in weights]
-        + [dma((2,)), dma((sides,)), dma((sides,))]
+        + [dma((2 + SMALL,)), dma((sides,)), dma((sides,))]
         + [dma((len(fine.halo),))] * 2
         + [dma((len(coarse.halo),))] * 2
-        + gather_scratch(units, split),
+        + gather_scratch(units),
         compiler_params=pltpu.CompilerParams(collective_id=1, has_side_effects=True, vmem_limit_bytes=LIMIT),
         name="levels",
     )(
-        tokens.reshape(fine.own, width), fine_tags.reshape(lat_len, 1, lon_len),
-        coarse_tags.reshape(coarse.lat_len, 1, coarse.lon_len), fine_gain[None], merge_gain[None], coarse_gain[None],
-        fine_table, coarse_table, index, offset_numbers(), lane, *weights,
+        tokens.reshape(fine.own, width), *small, *weights,
     )
     return fine_out.reshape(tokens.shape), coarse_out[None]
 

time: 88.5 us -> 82.1 us (0.928); the launches traced: 86.9 us -> 81.6 us
  Pallas kernels: 83.8 us -> 78.6 us
    pallas_call x1, Pallas kernels: 83.8 us -> 78.6 us  [shards(): pl.pallas_call(functools.partial(kernel, fine, coarse, units, split), out...]
where the time goes in v3:
time: 82.1 us; the launch traced here: 81.6 us
  Pallas kernels  78.6 us (96%)
  local copies, waits for them, and re-layouts  2.41 us (3%)
    pallas_call x1, Pallas kernels, shards(): pl.pallas_call(functools.partial(kernel, fine, coarse, units, split), out...  78.6 us
    unnamed x4, local copies, waits for them, and re-layouts  2.41 us

profile of v3, /device:TPU:0, one launch (start us, length us, event | category | flops | bytes accessed | tf_op | source)
XLA Modules:
  0.0 81.6 jit_solution(10491761455642412486)
XLA Ops:
  0.6 78.6 %levels.1 = (bf16[288,512]{1,0:T(8,128)(2,1)}, bf16[6,12,1024]{2,1,0:T(8,128)(2,1)}) custom-call(bf16[288,512]{1,0:T(8,128)(2,1)} %bitcast.12, s32[12,1,24]{2,1,0:T(1,128)} %bitcast.18, s32[6,1,12]{2,1,0:T(1,128)} %bitcast.20, s32[2,768]{1,0:T(2,128)} %constant.6.clone.refs_2_, f32[1,512]{1,0:T(1,128)} %bitcast.21, s32[512,4]{1,0:T(8,128)} %constant.7.clone.refs_4_, ...), custom_call_target="tpu_custom_call" | custom-call | tf_op jit(solution)/shard_map/levels/pallas_call | solution.py:763
  79.2 0.0 copy-start
  79.2 1.7 %copy.20 = bf16[1,12,24,512]{3,2,1,0:T(8,128)(2,1)} copy(bf16[1,12,24,512]{3,2,1,0:T(8,128)(2,1)} %bitcast.13) | data formatting | bytes 589824
  81.0 0.0 copy-done
  81.0 0.7 copy.21
Async XLA Ops:
  79.2 1.7 %copy-start = (bf16[6,12,1024]{2,1,0:T(8,128)(2,1)S(1)}, bf16[6,12,1024]{2,1,0:T(8,128)(2,1)}, u32[]{:S(2)}) copy-start(bf16[6,12,1024]{2,1,0:T(8,128)(2,1)} %get-tuple-element.5) | copy-start | bytes 442372

commit v4 on v3

--- a/solution.py
+++ b/solution.py
@@ -30,7 +30,7 @@
 AHEAD = 3
 LAG = 2
 RELAYED = 3
-ORDER = (2, 1, 3)
+ORDER = (1, 3, 2)
 MERGE = 256
 LAST = 256
 SMALL = 10
@@ -168,9 +168,15 @@
         )
 
     def clear(self):
-        for _, r, c, _ in self.plan.halo:
-            rows = pl.ds(self.plan.spot(r, c) * ROWS, ROWS)
-            self.wide[rows, :] = jnp.zeros((ROWS, self.wide.shape[1]), self.wide.dtype)
+        for side, r, c, _ in self.plan.halo:
+            start, dy = self.plan.spot(r, c) * ROWS, AROUND[side][0]
+            if SENT < ROWS:
+                spare = pl.ds(start + SENT, ROWS - SENT)
+                self.wide[spare, :] = jnp.zeros((ROWS - SENT, self.wide.shape[1]), self.wide.dtype)
+            if dy:
+                def beyond(start=start):
+                    self.wide[pl.ds(start, SENT), :] = jnp.zeros((SENT, self.wide.shape[1]), self.wide.dtype)
+                pl.when(jnp.logical_not(self.around.there(dy)))(beyond)
 
     def start(self):
         for n, (side, *_) in enumerate(self.plan.halo):
@@ -335,12 +341,12 @@
         for _ in range(times):
             k, count = self.now, len(self.units)
             self.now += 1
-            if k < count:
-                self.arrive()
             if 0 <= k - LAG < count:
                 self.forward()
             if 0 <= k - 2 * LAG < count:
                 self.share()
+            if k < count:
+                self.arrive()
             self.relay(k + 1)
 
     def ready(self, u):
@@ -522,11 +528,8 @@
     lons, lvls = lax.axis_size("lon"), lax.axis_size("lvl")
     gather = Gather((s0, s1, s2, s3, s4), (f0, f1, f2, f3, f4), units, split, sems)
     block_of = gather.block_of
-    tag_wide[...] = jnp.zeros_like(tag_wide)
     halo = Halo(around, fine, own, wide, send1, recv1)
     halo_two = Halo(around, coarse, two_own, two_wide, send2, recv2)
-    halo.clear()
-    halo_two.clear()
     barrier = pltpu.get_barrier_semaphore()
     peers = around.greet(barrier) + gather.greet(barrier)
     brought = (
@@ -540,6 +543,13 @@
     fetch.start()
     for other in fetches[3:]:
         other.start()
+    halo.clear()
+    halo_two.clear()
+    for side, (dy, dx) in enumerate(AROUND):
+        if dy:
+            def clear(side=side):
+                tag_wide[side] = jnp.zeros(tag_wide.shape[1:], tag_wide.dtype)
+            pl.when(jnp.logical_not(around.there(dy)))(clear)
     pl.semaphore_wait(barrier, peers)
     gather.begin()
     for other in fetches[:3]:
@@ -717,6 +727,19 @@
         around.when_there(-dy, lambda side=side: tag_copy(side).wait_send())
     halo.drain()
     halo_two.drain()
+
+
+def publish_kernel(fine_in, coarse_in, fine_out, coarse_out, fine_held, coarse_held, sems):
+    steps = ((fine_in, fine_held, fine_out), (coarse_in, coarse_held, coarse_out))
+    come = [pltpu.make_async_copy(a, b, sems.at[n]) for n, (a, b, _) in enumerate(steps)]
+    leave = [pltpu.make_async_copy(b, c, sems.at[2 + n]) for n, (_, b, c) in enumerate(steps)]
+    for copy in come:
+        copy.start()
+    for n in range(2):
+        come[n].wait()
+        leave[n].start()
+    for copy in leave:
+        copy.wait()
 
 
 def level_scratch(plan, features, heads):
@@ -789,6 +812,14 @@
     )(
         tokens.reshape(fine.own, width), *small, *weights,
     )
+    fine_out, coarse_out = pl.pallas_call(
+        publish_kernel,
+        out_shape=[jax.ShapeDtypeStruct(x.shape, x.dtype) for x in (fine_out, coarse_out)],
+        in_specs=[HBM] * 2,
+        out_specs=[HBM] * 2,
+        scratch_shapes=[pltpu.VMEM(x.shape, x.dtype) for x in (fine_out, coarse_out)] + [dma((4,))],
+        name="publish",
+    )(fine_out, coarse_out)
     return fine_out.reshape(tokens.shape), coarse_out[None]
 
 

time: 82.1 us -> 79.8 us (0.972)
  local copies, waits for them, and re-layouts: 2.41 us -> 0 us
    unnamed x4 -> x0, local copies, waits for them, and re-layouts: 2.41 us -> none
    pallas_call x0 -> x1, Pallas kernels: none -> 1.77 us  [shards(): pl.pallas_call(publish_kernel, out_shape=[jax.ShapeDtypeStruct(x.shape, x...]
    pallas_call x1, Pallas kernels: 78.6 us -> 77.1 us  [shards(): pl.pallas_call(functools.partial(kernel, fine, coarse, units, split), out...]
where the time goes in v4:
time: 79.8 us; the launch traced here: 79.7 us
  Pallas kernels  78.9 us (99%)
  between operations  0.8 us (1%)
    pallas_call x1, Pallas kernels, shards(): pl.pallas_call(functools.partial(kernel, fine, coarse, units, split), out...  77.1 us
    pallas_call x1, Pallas kernels, shards(): pl.pallas_call(publish_kernel, out_shape=[jax.ShapeDtypeStruct(x.shape, x...  1.77 us

profile of v4, /device:TPU:0, one launch (start us, length us, event | category | flops | bytes accessed | tf_op | source)
XLA Modules:
  0.0 79.7 jit_solution(12948655910164553684)
XLA Ops:
  0.6 77.1 %levels.1 = (bf16[288,512]{1,0:T(8,128)(2,1)}, bf16[6,12,1024]{2,1,0:T(8,128)(2,1)}) custom-call(bf16[288,512]{1,0:T(8,128)(2,1)} %bitcast.12, s32[12,1,24]{2,1,0:T(1,128)} %bitcast.16, s32[6,1,12]{2,1,0:T(1,128)} %bitcast.18, s32[2,768]{1,0:T(2,128)} %constant.6.clone.refs_2_, f32[1,512]{1,0:T(1,128)} %bitcast.19, s32[512,4]{1,0:T(8,128)} %constant.7.clone.refs_4_, ...), custom_call_target="tpu_custom_call" | custom-call | tf_op jit(solution)/shard_map/levels/pallas_call | solution.py:786
  77.8 1.8 %publish.1 = (bf16[288,512]{1,0:T(8,128)(2,1)}, bf16[6,12,1024]{2,1,0:T(8,128)(2,1)}) custom-call(bf16[288,512]{1,0:T(8,128)(2,1)} %get-tuple-element.6.fine_in, bf16[6,12,1024]{2,1,0:T(8,128)(2,1)} %get-tuple-element.7.coarse_in), custom_call_target="tpu_custom_call" | custom-call | tf_op jit(solution)/shard_map/publish/pallas_call | solution.py:815

commit v5 on v4

--- a/solution.py
+++ b/solution.py
@@ -179,7 +179,7 @@
                 pl.when(jnp.logical_not(self.around.there(dy)))(beyond)
 
     def start(self):
-        for n, (side, *_) in enumerate(self.plan.halo):
+        for n, (side, *_) in sorted(enumerate(self.plan.halo), key=lambda item: -abs(AROUND[item[1][0]][0])):
             self.around.when_there(-AROUND[side][0], lambda n=n: self.copy(n).start())
 
     def finish(self):

time: 79.8 us -> 79.8 us (level)
  no operation moved by 1% of the time
where the time goes in v5:
time: 79.8 us; the launch traced here: 79.7 us
  Pallas kernels  78.9 us (99%)
  between operations  0.8 us (1%)
    pallas_call x1, Pallas kernels, shards(): pl.pallas_call(functools.partial(kernel, fine, coarse, units, split), out...  77.1 us
    pallas_call x1, Pallas kernels, shards(): pl.pallas_call(publish_kernel, out_shape=[jax.ShapeDtypeStruct(x.shape, x...  1.77 us

profile of v5, /device:TPU:0, one launch (start us, length us, event | category | flops | bytes accessed | tf_op | source)
XLA Modules:
  0.0 79.7 jit_solution(2685088491386636746)
XLA Ops:
  0.6 77.1 %levels.1 = (bf16[288,512]{1,0:T(8,128)(2,1)}, bf16[6,12,1024]{2,1,0:T(8,128)(2,1)}) custom-call(bf16[288,512]{1,0:T(8,128)(2,1)} %bitcast.12, s32[12,1,24]{2,1,0:T(1,128)} %bitcast.16, s32[6,1,12]{2,1,0:T(1,128)} %bitcast.18, s32[2,768]{1,0:T(2,128)} %constant.6.clone.refs_2_, f32[1,512]{1,0:T(1,128)} %bitcast.19, s32[512,4]{1,0:T(8,128)} %constant.7.clone.refs_4_, ...), custom_call_target="tpu_custom_call" | custom-call | tf_op jit(solution)/shard_map/levels/pallas_call | solution.py:786
  77.8 1.8 %publish.1 = (bf16[288,512]{1,0:T(8,128)(2,1)}, bf16[6,12,1024]{2,1,0:T(8,128)(2,1)}) custom-call(bf16[288,512]{1,0:T(8,128)(2,1)} %get-tuple-element.6.fine_in, bf16[6,12,1024]{2,1,0:T(8,128)(2,1)} %get-tuple-element.7.coarse_in), custom_call_target="tpu_custom_call" | custom-call | tf_op jit(solution)/shard_map/publish/pallas_call | solution.py:815
